TPU v7x, 128 devices: a whole 4x4x4 slice. The times are simulated.
128 devices in a mesh: shell: 4 (over y_hi, core), img: 32 (over z, y_lo, x).
Axes of the slice: x: 4, y: 4 (y_hi: 2, y_lo: 2; y = y_hi * 2 + y_lo), z: 4, core: 2. Of those that a mesh axis runs over, the one named last changes fastest.
Arguments:
- images: bfloat16 [24576, 16384], P('img', 'shell'), may hold values from -12 to 12, as said below
- references: bfloat16 [1024, 16384], P('img', 'shell'), may hold values from -1 to 1, as said below
- shell_of_pixel: int32 [16384], P('shell'), may hold values from 0 to 63
- noise_power: float32 [64], replicated, may hold values from 0.1 to 10
- ref_class: int32 [1024], replicated, may hold values from 0 to 3
- ref_orient: int32 [1024], replicated, may hold values from 0 to 6143
- class_logw: float32 [4], replicated, may hold values from -4 to 4
- orient_logw: float32 [6144], replicated, may hold values from -4 to 4
Outputs:
- accumulators: float32 [1024, 16384], P('img', 'shell')
- evidence_logarithm: float32 [24576], P('img')
Inputs may be any that keep to these rules, and one draw needn't show every extreme that they name: `images`: images are real-valued Fourier data. `references`: references are real-valued projections.
All inputs are finite; a program needn't handle non-finite values.
Results may differ from a plain program's by a relative error of at most 0.0077.
Values may be sent and summed in bfloat16 or wider, within the bound.
A program may use at most 128 MiB of HBM per device.

v0:
```python
import jax
import jax.numpy as jnp
from jax import lax
from jax.sharding import PartitionSpec as P

inverse_heat_factor = 0.5


def split_up(array, dim, peers):
    dims = array.shape
    tiles = array.reshape(*dims[:dim], peers, dims[dim] // peers, *dims[dim + 1 :])
    return jnp.moveaxis(tiles, dim, 0)


def sum_at_owner(array, axis, dim):
    peers = lax.axis_size(axis)
    tiles = lax.all_to_all(split_up(array, dim, peers), axis, 0, 0, tiled=True)
    return jnp.sum(tiles, axis=0)


def sent_to_all(array, axis):
    peers = lax.axis_size(axis)
    return lax.all_to_all(
        jnp.broadcast_to(array[None], (peers, *array.shape)), axis, 0, 0, tiled=True
    )


def in_order(tiles, dim):
    dims = list(tiles.shape[1:])
    dims[dim] *= tiles.shape[0]
    return jnp.moveaxis(tiles, 0, dim).reshape(dims)


def gathered_copies(array, axis, dim):
    tiles = sent_to_all(array, axis)
    return in_order(tiles, dim)


def tempered_softmax(overall_total, beforehand_logarithmic_share):
    raw_logarithmic_measures = (
        inverse_heat_factor * overall_total + beforehand_logarithmic_share[None, :]
    )
    highest = jnp.max(raw_logarithmic_measures, axis=1)
    evidence_logarithm = highest + jnp.log(
        jnp.sum(jnp.exp(raw_logarithmic_measures - highest[:, None]), axis=1)
    )
    posterior = jnp.exp(raw_logarithmic_measures - evidence_logarithm[:, None]).astype(jnp.bfloat16)
    return (posterior, evidence_logarithm)


def shards(
    images, references, shell_of_pixel, noise_power, ref_class, ref_orient, class_logw, orient_logw
):
    inverse_noise = 1.0 / noise_power
    matches = shell_of_pixel[:, None] == jnp.arange(noise_power.shape[0], dtype=jnp.int32)[None, :]
    weights = jnp.sum(jnp.where(matches, inverse_noise[None, :], jnp.float32(0.0)), axis=1)
    weighted = (images.astype(jnp.float32) * weights[None, :]).astype(jnp.bfloat16)
    reference_block_list = lax.all_gather(references, "img", axis=0, tiled=True)
    correlation = lax.dot_general(
        weighted, reference_block_list, (((1,), (1,)), ((), ())), preferred_element_type=jnp.float32
    )
    block_float = reference_block_list.astype(jnp.float32)
    ref_norm = jnp.dot(block_float * block_float, weights, precision=lax.Precision.HIGHEST)
    incomplete_measures = correlation - 0.5 * ref_norm[None, :]
    class_agreement = (
        ref_class[:, None] == jnp.arange(class_logw.shape[0], dtype=jnp.int32)[None, :]
    )
    beforehand_logarithmic_share = (
        jnp.sum(jnp.where(class_agreement, class_logw[None, :], jnp.float32(0.0)), axis=1)
        + orient_logw[ref_orient]
    )
    score_rows = sum_at_owner(incomplete_measures, "shell", 0)
    row_posterior, row_log_marginal = tempered_softmax(score_rows, beforehand_logarithmic_share)
    posterior, evidence_logarithm = (
        gathered_copies(row_posterior, "shell", 0),
        gathered_copies(row_log_marginal.astype(jnp.bfloat16), "shell", 0).astype(
            row_log_marginal.dtype
        ),
    )
    accumulators = lax.psum_scatter(
        lax.dot_general(
            posterior, images, (((0,), (0,)), ((), ())), preferred_element_type=jnp.float32
        ),
        "img",
        scatter_dimension=0,
        tiled=True,
    )
    return (accumulators, evidence_logarithm)


def solution(mesh):
    placed = (P("img", "shell"), P("img", "shell"), P("shell"), P(), P(), P(), P(), P())
    return jax.shard_map(
        shards, mesh=mesh, in_specs=placed, out_specs=(P("img", "shell"), P("img")), check_vma=False
    )
```

profile of v0, /device:TPU:8, one launch (start us, length us, event | category | flops | bytes accessed | tf_op | source)
XLA Modules:
  0.0 493.9 jit_solution(11843192143524128233)
XLA Ops:
  7.2 0.0 copy-start
  7.2 0.0 all-gather.2.cloned.1.call-start
  7.2 0.7 all-gather.2.cloned.1.call-update
  7.9 0.7 broadcast_divide_fusion
  8.6 1.0 select_reduce_fusion
  9.5 162.2 %all-gather.2.cloned.1.call-done = bf16[1024,4096]{1,0:T(8,128)(2,1)} async-done(((bf16[32,4096]{1,0:T(8,128)(2,1)}), bf16[1024,4096]{1,0:T(8,128)(2,1)}) %all-gather.2.cloned.1.call-update) | async-done | bytes 8388624 | tf_op jit(solution)/shard_map/all_gather | solution.py:58
  171.7 0.0 copy-start.1
  171.7 18.0 %fusion = f32[1,1024]{1,0:T(1,128)S(1)} fusion(f32[4096,1]{0,1:T(1,128)S(1)} %bitcast.10, bf16[1024,4096]{1,0:T(8,128)(2,1)} %all-gather.2.cloned.1.call-done), kind=kOutput, calls=%fused_computation.1 | convolution fusion | flops 58720256 | bytes 8409088 | tf_op jit(solution)/shard_map/dot_general | solution.py:63
  189.7 0.0 copy-done.1
  189.8 10.3 %fusion.5 = f32[768,1024]{1,0:T(8,128)} fusion(bf16[1024,4096]{1,0:T(8,128)(2,1)S(1)} %copy-done.1, bf16[768,4096]{1,0:T(8,128)(2,1)} %param.8, f32[4096]{0:T(1024)S(1)} %select_reduce_fusion, f32[1024]{0:T(1024)S(1)} %broadcast_multiply_fusion), kind=kOutput, calls=%fused_computation.7 | convolution fusion | flops 6452674560 | bytes 17846272 | tf_op jit(solution)/shard_map/dot_general | solution.py:59
  200.0 0.0 copy-start.2
  200.0 0.0 copy-start.3
  200.0 0.0 copy-start.4
  200.0 3.8 all-to-all-start
  203.9 0.0 reduce-scatter.2.cloned.1.call-start
  203.9 0.0 copy-done.2
  204.0 0.0 copy-done
  204.0 6.2 %gather_fusion = f32[1024]{0:T(1024)S(1)} fusion(f32[6144]{0:T(1024)S(1)} %copy-done, s32[1024]{0:T(1024)S(1)} %fusion.7), kind=kCustom, calls=%fused_computation | custom fusion | bytes 12288 | tf_op jit(solution)/shard_map/gather | solution.py:70
  210.1 0.0 copy-done.3
  210.1 0.0 copy-done.4
  210.1 0.1 select_reduce_fusion.1
  210.2 32.0 %all-to-all-done = f32[4,192,1024]{2,1,0:T(8,128)S(1)} async-done(((f32[4,192,1024]{2,1,0:T(8,128)}), f32[4,192,1024]{2,1,0:T(8,128)S(1)}, u32[]{:S(2)}, u32[]{:S(2)}) %all-to-all-start) | async-done | bytes 3145760 | tf_op jit(solution)/shard_map/all_to_all | solution.py:17
  242.3 1.2 reduce_sum.37
  243.5 1.3 fusion.6
  244.8 1.4 exponential_reduce_fusion
  246.2 1.3 exponential_convert_fusion
  247.5 0.2 broadcast_in_dim.35
  247.7 24.0 %all_to_all.16 = bf16[4,192,1024]{2,1,0:T(8,128)(2,1)S(1)} all-to-all(bf16[4,192,1024]{2,1,0:T(8,128)(2,1)S(1)} %broadcast_in_dim.35), channel_id=1, replica_groups=mesh['shell'=4,'img'=32] {'shell'}, dimensions={0} | all-to-all | bytes 3145728 | tf_op jit(solution)/shard_map/all_to_all | solution.py:23
  271.7 13.0 %fusion.9 = f32[1024,4096]{1,0:T(8,128)} fusion(bf16[768,1024]{1,0:T(8,128)(2,1)S(1)} %bitcast.8, bf16[768,4096]{1,0:T(8,128)(2,1)} %param.8), kind=kOutput, calls=%fused_computation.23 | convolution fusion | flops 6442450944 | bytes 24641536 | tf_op jit(solution)/shard_map/dot_general | solution.py:81
  284.7 0.0 reduce-scatter.2.cloned.1.call-update
  284.8 7.6 %all_to_all.17 = bf16[4,1,192]{2,1,0:T(2,128)(2,1)S(1)} all-to-all(bf16[4,1,192]{2,1,0:T(2,128)(2,1)S(1)} %broadcast_in_dim.56), channel_id=1, replica_groups=mesh['shell'=4,'img'=32] {'shell'}, dimensions={0} | all-to-all | bytes 3072 | tf_op jit(solution)/shard_map/all_to_all | solution.py:23
  292.4 0.7 reshape.81
  293.1 194.0 %reduce-scatter.2.cloned.1.call-done = f32[32,4096]{1,0:T(8,128)} async-done(((f32[1024,4096]{1,0:T(8,128)}), f32[32,4096]{1,0:T(8,128)}) %reduce-scatter.2.cloned.1.call-update) | async-done | bytes 524304 | tf_op jit(solution)/shard_map/reduce_scatter | solution.py:80
  (6 shorter events, 0.1 us)
Async XLA Ops:
  7.2 196.8 %copy-start = (f32[6144]{0:T(1024)S(1)}, f32[6144]{0:T(1024)}, u32[]{:S(2)}) copy-start(f32[6144]{0:T(1024)} %param.15) | copy-start | bytes 73732
  7.2 164.5 %all-gather.2.cloned.1.call-start = ((), (), s32[]{:S(2)}) async-start(), calls=%async_computation.4 | async-start | bytes 8650752 | tf_op jit(solution)/shard_map/all_gather | solution.py:58
  171.7 18.0 %copy-start.1 = (bf16[1024,4096]{1,0:T(8,128)(2,1)S(1)}, bf16[1024,4096]{1,0:T(8,128)(2,1)}, u32[]{:S(2)}) copy-start(bf16[1024,4096]{1,0:T(8,128)(2,1)} %all-gather.2.cloned.1.call-done) | copy-start | bytes 25165828
  200.0 3.9 copy-start.2
  200.0 10.1 %copy-start.3 = (s32[1024]{0:T(1024)S(1)}, s32[1024]{0:T(1024)}, u32[]{:S(2)}) copy-start(s32[1024]{0:T(1024)} %param.12) | copy-start | bytes 12292
  200.0 10.1 %copy-start.4 = (f32[4]{0:T(128)S(1)}, f32[4]{0:T(128)}, u32[]{:S(2)}) copy-start(f32[4]{0:T(128)} %param.14) | copy-start | bytes 52
  200.0 42.2 %all-to-all-start = ((f32[4,192,1024]{2,1,0:T(8,128)}), f32[4,192,1024]{2,1,0:T(8,128)S(1)}, u32[]{:S(2)}, u32[]{:S(2)}) async-start(f32[4,192,1024]{2,1,0:T(8,128)} %bitcast.9), calls=%async_computation | async-start | bytes 6291456 | tf_op jit(solution)/shard_map/all_to_all | solution.py:17
  203.9 283.2 %reduce-scatter.2.cloned.1.call-start = ((), (), s32[]{:S(2)}) async-start(), calls=%async_computation.5 | async-start | bytes 17301504 | tf_op jit(solution)/shard_map/reduce_scatter | solution.py:80
Sparse Core Ops, SparseCore 0:
  9.6 162.0 all-gather.1
  284.9 202.1 reduce-scatter.1
where the time goes:
time: 502 us; the launch traced here: 494 us
  waiting for transfers between devices  389 us (77%)
  matrix products  41.3 us (8%)
  blocking collectives  31.6 us (6%)
  between operations  14.1 us (3%)
  local copies, waits for them, and re-layouts  7.06 us (1%)
  other arithmetic  7 us (1%)
    reduce_scatter x1, waiting for transfers between devices, shards(): lax.psum_scatter(lax.dot_general(posterior, images, (((0,), (0,)), ((), (...  194 us
    all_gather x1, waiting for transfers between devices, shards(): reference_block_list = lax.all_gather(references, 'img', axis=0, tiled=True)  162 us
    all_to_all x1, waiting for transfers between devices, sum_at_owner(): tiles = lax.all_to_all(split_up(array, dim, peers), axis, 0, 0, tiled=True)  32 us
    all_to_all x2, blocking collectives, sent_to_all(): lax.all_to_all(jnp.broadcast_to(array[None], (peers, *array.shape)), axis...  31.6 us
    dot_general x1, matrix products, shards(): jnp.dot(block_float * block_float, weights, precision=lax.Precision.HIGHEST)  18 us
    dot_general x1, matrix products, shards(): lax.dot_general(posterior, images, (((0,), (0,)), ((), ())), preferred_el...  13 us
    dot_general x1, matrix products, shards(): lax.dot_general(weighted, reference_block_list, (((1,), (1,)), ((), ())),...  10.3 us
  transfers between devices with their start and end apart: 3, of which 3 were waited for; matrix products, arithmetic and copies ran while one was open for 2% of the time, Pallas kernels for 0%

commit v1 on v0

v1 whole, which is shorter than its diff:
```python
import jax
import jax.numpy as jnp
from jax import lax
from jax.experimental import pallas as pl
from jax.experimental.pallas import tpu as pltpu
from jax.sharding import PartitionSpec as P

INVERSE_HEAT = 0.5
MESH = pl.DeviceIdType.MESH
F32 = jnp.float32
BF16 = jnp.bfloat16

NZ, NY, NX = 4, 2, 4
ROWS = 32
PIECE = 16
PIX = 4096
NIM = 768
HALF = NIM // 2
GROUP = 256
SIDE = GROUP // 2
NREF = 1024
TILE = 512
NT = PIX // TILE
PH = PIX // 2
NORIENT = 6144


def kernel(
    images_hbm,
    references_hbm,
    shell_ref,
    noise_ref,
    key_ref,
    orient_ref,
    class_ref,
    out_ref,
    evidence_ref,
    im,
    wim,
    refs,
    score,
    core_in,
    row_out,
    row_in,
    total,
    weight,
    keys,
    prior,
    stat_out,
    stat_in,
    post,
    s1,
    s2,
    s3,
    r_opp,
    r_plus,
    r_minus,
    acc,
    z1,
    z2,
    z3,
    zr_opp,
    zr_plus,
    zr_minus,
    y_out,
    y_in,
    load_sem,
    ag_s,
    ag_r,
    ex_s,
    ex_r,
    a_s,
    a_r,
    b_s,
    b_r,
    yy_s,
    yy_r,
):
    s = lax.axis_index("shell")
    i = lax.axis_index("img")
    core = lax.rem(s, 2)
    y_hi = s // 2
    z = i // (NY * NX)
    y = lax.rem(i // NX, NY)
    x = lax.rem(i, NX)

    def at(zz, yv, xx):
        return (zz * NY + yv) * NX + xx

    x_plus = (s, at(z, y, lax.rem(x + 1, NX)))
    x_minus = (s, at(z, y, lax.rem(x + NX - 1, NX)))
    z_plus = (s, at(lax.rem(z + 1, NZ), y, x))
    z_minus = (s, at(lax.rem(z + NZ - 1, NZ), y, x))
    y_pal = (s, at(z, 1 - y, x))
    core_pal = (y_hi * 2 + 1 - core, i)
    hi_pal = ((1 - y_hi) * 2 + core, i)
    a_plus, a_minus = (x_plus, z_plus), (x_minus, z_minus)
    b_plus, b_minus = (z_plus, x_plus), (z_minus, x_minus)

    def remote(src, dst, send_sem, recv_sem, peer):
        return pltpu.make_async_remote_copy(
            src_ref=src,
            dst_ref=dst,
            send_sem=send_sem,
            recv_sem=recv_sem,
            device_id=peer,
            device_id_type=MESH,
        )

    def landed(dst, send_sem, recv_sem):
        remote(dst, dst, send_sem, recv_sem, core_pal).wait_recv()

    own = []
    for t in range(2):
        c = pltpu.make_async_copy(
            references_hbm.at[pl.ds(t * PIECE, PIECE), :],
            refs.at[0, pl.ds(t * SIDE, PIECE), :],
            load_sem.at[t],
        )
        c.start()
        own.append(c)
    image_loads = []
    for n in range(3):
        c = pltpu.make_async_copy(
            images_hbm.at[pl.ds(n * 256, 256), :], im.at[pl.ds(n * 256, 256), :], load_sem.at[2 + n]
        )
        c.start()
        image_loads.append(c)

    barrier = pltpu.get_barrier_semaphore()
    for peer in (x_plus, x_minus, z_plus, z_minus, y_pal, core_pal, hi_pal):
        pl.semaphore_signal(barrier, inc=1, device_id=peer, device_id_type=MESH)
    pl.semaphore_wait(barrier, 7)

    index = {}
    ag_sends = []

    def slot(name):
        if name not in index:
            index[name] = len(index)
        return index[name]

    def piece(t, a, b, yr, part=None):
        rows = pl.ds(t * SIDE + b * 32 + yr * PIECE, PIECE)
        if part is None:
            return refs.at[a, rows, :]
        return refs.at[a, rows, pl.ds(part * PH, PH)]

    def ag_send(name, src, dst, peer):
        n = slot(name)
        c = remote(src, dst, ag_s.at[n], ag_r.at[n], peer)
        c.start()
        ag_sends.append(c)

    def ag_wait(name, dst):
        n = slot(name)
        landed(dst, ag_s.at[n], ag_r.at[n])

    def send_b(t, yr):
        ag_send(("b+", t, yr), piece(t, 0, 0, yr), piece(t, 0, 3, yr), b_plus[t])
        ag_send(("b-", t, yr), piece(t, 0, 0, yr), piece(t, 0, 1, yr), b_minus[t])

    def send_a(t, b, yr):
        ag_send(("a+", t, b, yr), piece(t, 0, b, yr), piece(t, 3, b, yr), a_plus[t])
        ag_send(("a-", t, b, yr), piece(t, 0, b, yr), piece(t, 1, b, yr), a_minus[t])

    for t in range(2):
        own[t].wait()
    for t in range(2):
        ag_send(("y", t), piece(t, 0, 0, 0), piece(t, 0, 0, 1), y_pal)
    for t in range(2):
        send_b(t, 0)
    for t in range(2):
        send_a(t, 0, 0)

    noise_row = 1.0 / noise_ref[...]
    r64 = lax.broadcasted_iota(jnp.int32, (64, 64), 0)
    c64 = lax.broadcasted_iota(jnp.int32, (64, 64), 1)
    noise_col = jnp.sum(
        jnp.where(r64 == c64, jnp.broadcast_to(noise_row, (64, 64)), 0.0), axis=1, keepdims=True
    )

    @pl.loop(0, PIX // 512)
    def _(n):
        cols = pl.ds(pl.multiple_of(n * 512, 512), 512)
        shell = jnp.broadcast_to(shell_ref[:, cols], (64, 512))
        hit = shell == lax.broadcasted_iota(jnp.int32, (64, 512), 0)
        weight[:, cols] = jnp.sum(
            jnp.where(hit, jnp.broadcast_to(noise_col, (64, 512)), 0.0), axis=0, keepdims=True
        )

    for t in range(2):
        ag_wait(("y", t), piece(t, 0, 0, 1))
        send_b(t, 1)
    for t in range(2):
        send_a(t, 0, 1)

    for n in range(3):
        image_loads[n].wait()

        @pl.loop(n * 16, n * 16 + 16)
        def _(k):
            rows = pl.ds(pl.multiple_of(k * 16, 16), 16)
            wim[rows, :] = (im[rows, :].astype(F32) * weight[...]).astype(BF16)

    for yr in range(2):
        for t in range(2):
            ag_wait(("b+", t, yr), piece(t, 0, 3, yr))
            ag_send(("bf+", t, yr), piece(t, 0, 3, yr, 0), piece(t, 0, 2, yr, 0), b_plus[t])
            ag_wait(("b-", t, yr), piece(t, 0, 1, yr))
            ag_send(("bf-", t, yr), piece(t, 0, 1, yr, 1), piece(t, 0, 2, yr, 1), b_minus[t])
        for t in range(2):
            send_a(t, 3, yr)
            send_a(t, 1, yr)
        if yr == 0:
            for a in range(4):
                for b in range(4):
                    for yr2 in range(2):
                        za = lax.rem(z + jnp.where(y_hi == 0, b, a), NZ)
                        xa = lax.rem(x + jnp.where(y_hi == 0, a, b), NX)
                        ya = y if yr2 == 0 else 1 - y
                        first = at(za, ya, xa) * ROWS + y_hi * PIECE
                        keys[pl.ds(a * SIDE + b * 32 + yr2 * PIECE, PIECE), :] = key_ref[
                            pl.ds(pl.multiple_of(first, PIECE), PIECE), :
                        ]

            @pl.loop(0, 4)
            def _(a):
                rows = pl.ds(pl.multiple_of(a * SIDE, SIDE), SIDE)
                key = keys[rows, :]
                orient = jnp.broadcast_to(lax.rem(key, 8192), (SIDE, 128))
                kind = key // 8192

                def add(n, sums):
                    cols = pl.ds(pl.multiple_of(n * 128, 128), 128)
                    ids = lax.broadcasted_iota(jnp.int32, (SIDE, 128), 1) + n * 128
                    logw = jnp.broadcast_to(orient_ref[:, cols], (SIDE, 128))
                    return sums + jnp.where(orient == ids, logw, 0.0)

                sums = lax.fori_loop(0, NORIENT // 128, add, jnp.zeros((SIDE, 128), F32))
                found = jnp.zeros((SIDE, 1), F32)
                for n in range(4):
                    found = found + jnp.where(kind == n, class_ref[n], 0.0)
                prior[rows, :] = found + jnp.sum(sums, axis=1, keepdims=True)

    for yr in range(2):
        for t in range(2):
            ag_wait(("bf+", t, yr), piece(t, 0, 2, yr, 0))
            ag_wait(("bf-", t, yr), piece(t, 0, 2, yr, 1))
            send_a(t, 2, yr)

    mine = pl.ds(pl.multiple_of(core * HALF, 128), HALF)
    theirs = pl.ds(pl.multiple_of((1 - core) * HALF, 128), HALF)
    keep = pl.ds(pl.multiple_of(y_hi * SIDE, SIDE), SIDE)
    give = pl.ds(pl.multiple_of((1 - y_hi) * SIDE, SIDE), SIDE)
    ex_sends = []

    def ex_send(n, src, dst, peer):
        c = remote(src, dst, ex_s.at[n], ex_r.at[n], peer)
        c.start()
        ex_sends.append(c)

    def ex_wait(n, dst):
        landed(dst, ex_s.at[n], ex_r.at[n])

    def do_scores(g):
        def add(n, sums):
            cols = pl.ds(pl.multiple_of(n * 128, 128), 128)
            r = refs[g, :, cols].astype(F32)
            return sums + r * r * weight[:, cols]

        sums = lax.fori_loop(0, PIX // 128, add, jnp.zeros((GROUP, 128), F32))
        norm = 0.5 * jnp.sum(sums, axis=1, keepdims=True)

        @pl.loop(0, 3)
        def _(n):
            rows = pl.ds(pl.multiple_of(n * 256, 256), 256)
            part = lax.dot_general(
                refs[g], wim[rows, :], (((1,), (1,)), ((), ())), preferred_element_type=F32
            )
            score[g, :, rows] = part - norm

        ex_send(g, score.at[g, :, theirs], core_in.at[g], core_pal)

    def do_rows(g):
        ex_wait(g, core_in.at[g])
        row_out[g] = score[g, give, mine] + core_in[g, give, :]
        ex_send(4 + g, row_out.at[g], row_in.at[g], hi_pal)
        total[g] = score[g, keep, mine] + core_in[g, keep, :]

    def do_logits(g):
        ex_wait(4 + g, row_in.at[g])
        rows = pl.ds(g * SIDE, SIDE)
        logits = INVERSE_HEAT * (total[g] + row_in[g]) + prior[rows, :]
        total[g] = logits
        return jnp.max(logits, axis=0, keepdims=True)

    do_scores(0)
    order = [(0, 0), (0, 1), (3, 0), (1, 0), (3, 1), (1, 1), (2, 0), (2, 1)]
    for n, (b, yr) in enumerate(order):
        for t in range(2):
            ag_wait(("a+", t, b, yr), piece(t, 3, b, yr))
            ag_send(("af+", t, b, yr), piece(t, 3, b, yr, 0), piece(t, 2, b, yr, 0), a_plus[t])
            ag_wait(("a-", t, b, yr), piece(t, 1, b, yr))
            ag_send(("af-", t, b, yr), piece(t, 1, b, yr, 1), piece(t, 2, b, yr, 1), a_minus[t])
        if n == 1:
            do_rows(0)
    do_scores(1)
    do_scores(3)
    do_rows(1)
    do_rows(3)
    for b, yr in order:
        for t in range(2):
            ag_wait(("af+", t, b, yr), piece(t, 2, b, yr, 0))
            ag_wait(("af-", t, b, yr), piece(t, 2, b, yr, 1))
    do_scores(2)
    top = do_logits(0)
    top = jnp.maximum(top, do_logits(1))
    do_rows(2)
    top = jnp.maximum(top, do_logits(3))
    top = jnp.maximum(top, do_logits(2))
    mass = jnp.zeros((1, HALF), F32)
    for g in range(4):
        mass = mass + jnp.sum(jnp.exp(total[g] - top), axis=0, keepdims=True)
    stat_out[0:8, :] = jnp.broadcast_to(top, (8, HALF))
    stat_out[8:16, :] = jnp.broadcast_to(mass, (8, HALF))
    ex_send(8, stat_out.at[0:16], stat_in.at[0:16], hi_pal)
    ex_wait(8, stat_in.at[0:16])
    other_top, other_mass = stat_in[0:1, :], stat_in[8:9, :]
    first = y_hi == 0
    top_a, top_b = jnp.where(first, top, other_top), jnp.where(first, other_top, top)
    mass_a, mass_b = jnp.where(first, mass, other_mass), jnp.where(first, other_mass, mass)
    best = jnp.maximum(top_a, top_b)
    evidence = best + jnp.log(mass_a * jnp.exp(top_a - best) + mass_b * jnp.exp(top_b - best))
    stat_out[16:24, :] = jnp.broadcast_to(evidence, (8, HALF))
    gs = (2, 1, 3, 0)
    for g in gs:
        post[g, keep, mine] = jnp.exp(total[g] - evidence).astype(BF16)
        ex_send(12 + g, post.at[g, keep, mine], post.at[g, keep, mine], hi_pal)
        ex_send(16 + g, post.at[g, keep, mine], post.at[g, keep, mine], core_pal)
    ex_send(9, stat_out.at[16:24], stat_in.at[16:24], core_pal)

    def do_relay(g):
        ex_wait(12 + g, post.at[g, give, mine])
        ex_send(20 + g, post.at[g, give, mine], post.at[g, give, mine], core_pal)

    def do_posterior(g):
        ex_wait(16 + g, post.at[g, keep, theirs])
        ex_wait(20 + g, post.at[g, give, theirs])

    def product(g, j):
        cols = pl.ds(pl.multiple_of(j * TILE, TILE), TILE)
        return jnp.dot(post[g], im[:, cols], preferred_element_type=F32)

    def half(t):
        return pl.ds(t * SIDE, SIDE)

    def a_copy(kind, j, t, src, dst, peer):
        return remote(
            src.at[j, half(t)], dst.at[j, half(t)], a_s.at[kind, j, t], a_r.at[kind, j, t], peer
        )

    def a_landed(kind, j, t, dst):
        landed(dst.at[j, half(t)], a_s.at[kind, j, t], a_r.at[kind, j, t])

    do_relay(2)
    do_posterior(2)
    do_relay(1)

    @pl.loop(0, 4)
    def _(k):
        s2[k] = product(2, k).astype(BF16)
        for t in range(2):
            a_copy(0, k, t, s2, r_opp, a_plus[t]).start()
        s2[k + 4] = product(2, k + 4).astype(BF16)
        for t in range(2):
            a_copy(0, k + 4, t, s2, r_opp, a_minus[t]).start()

    do_relay(3)
    do_posterior(1)
    do_posterior(3)
    do_relay(0)

    @pl.loop(0, 4)
    def _(k):
        s1[k + 4] = product(1, k + 4).astype(BF16)
        for t in range(2):
            a_copy(1, k + 4, t, s1, r_minus, a_plus[t]).start()
        s3[k] = product(3, k).astype(BF16)
        for t in range(2):
            a_copy(2, k, t, s3, r_plus, a_minus[t]).start()

    do_posterior(0)
    ex_wait(9, stat_in.at[16:24])
    evidence_ref[:, mine] = stat_out[16:17, :]
    evidence_ref[:, theirs] = stat_in[16:17, :]

    @pl.loop(0, 4)
    def _(k):
        p1 = product(1, k)
        for t in range(2):
            a_landed(0, k, t, r_opp)
        s1[k] = (p1 + r_opp[k].astype(F32)).astype(BF16)
        for t in range(2):
            a_copy(1, k, t, s1, r_minus, a_plus[t]).start()
        p3 = product(3, k + 4)
        for t in range(2):
            a_landed(0, k + 4, t, r_opp)
        s3[k + 4] = (p3 + r_opp[k + 4].astype(F32)).astype(BF16)
        for t in range(2):
            a_copy(2, k + 4, t, s3, r_plus, a_minus[t]).start()

    def b_copy(kind, j, t, src, dst, peer):
        return remote(src.at[j, t], dst.at[j, t], b_s.at[kind, j, t], b_r.at[kind, j, t], peer)

    def b_landed(kind, j, t, dst):
        landed(dst.at[j, t], b_s.at[kind, j, t], b_r.at[kind, j, t])

    def y_copy(j, t):
        return remote(y_out.at[j, t], y_in.at[j, t], yy_s.at[j, t], yy_r.at[j, t], y_pal)

    def step_a(k):
        for j, low in ((k, True), (k + 4, False)):
            p = product(0, j)
            for t in range(2):
                a_landed(1, j, t, r_minus)
                a_landed(2, j, t, r_plus)
            acc[j] = p + r_plus[j].astype(F32) + r_minus[j].astype(F32)
            for t in range(2):
                o = t * SIDE
                z2[j, t] = acc[j, o + 64 : o + 96, :].astype(BF16)
                b_copy(0, j, t, z2, zr_opp, b_plus[t] if low else b_minus[t]).start()
                if low:
                    z3[j, t] = acc[j, o + 96 : o + 128, :].astype(BF16)
                    b_copy(2, j, t, z3, zr_plus, b_minus[t]).start()
                else:
                    z1[j, t] = acc[j, o + 32 : o + 64, :].astype(BF16)
                    b_copy(1, j, t, z1, zr_minus, b_plus[t]).start()

    def step_b(k):
        for t in range(2):
            o = t * SIDE
            b_landed(0, k, t, zr_opp)
            z1[k, t] = (acc[k, o + 32 : o + 64, :] + zr_opp[k, t].astype(F32)).astype(BF16)
            b_copy(1, k, t, z1, zr_minus, b_plus[t]).start()
            j = k + 4
            b_landed(0, j, t, zr_opp)
            z3[j, t] = (acc[j, o + 96 : o + 128, :] + zr_opp[j, t].astype(F32)).astype(BF16)
            b_copy(2, j, t, z3, zr_plus, b_minus[t]).start()

    def step_c(k):
        for j in (k, k + 4):
            for t in range(2):
                o = t * SIDE
                b_landed(1, j, t, zr_minus)
                b_landed(2, j, t, zr_plus)
                v = acc[j, o : o + 32, :] + zr_plus[j, t].astype(F32) + zr_minus[j, t].astype(F32)
                y_out[j, t] = v[PIECE:, :].astype(BF16)
                y_copy(j, t).start()
                acc[j, o : o + PIECE, :] = v[:PIECE, :]

    def step_d(k):
        for j in (k, k + 4):
            for t in range(2):
                o = t * SIDE
                y_copy(j, t).wait_recv()
                cols = pl.ds(pl.multiple_of(j * TILE, TILE), TILE)
                out_ref[t * PIECE : (t + 1) * PIECE, cols] = acc[j, o : o + PIECE, :] + y_in[
                    j, t
                ].astype(F32)

    @pl.loop(0, 7)
    def _(k):
        @pl.when(k < 4)
        def _():
            step_a(k)

        @pl.when(jnp.logical_and(k >= 1, k < 5))
        def _():
            step_b(k - 1)

        @pl.when(jnp.logical_and(k >= 2, k < 6))
        def _():
            step_c(k - 2)

        @pl.when(k >= 3)
        def _():
            step_d(k - 3)

    for c in ag_sends:
        c.wait_send()
    for c in ex_sends:
        c.wait_send()

    @pl.loop(0, NT)
    def _(j):
        for t in range(2):
            a_copy(0, j, t, s2, r_opp, core_pal).wait_send()
            a_copy(1, j, t, s1, r_minus, core_pal).wait_send()
            a_copy(2, j, t, s3, r_plus, core_pal).wait_send()
            b_copy(0, j, t, z2, zr_opp, core_pal).wait_send()
            b_copy(1, j, t, z1, zr_minus, core_pal).wait_send()
            b_copy(2, j, t, z3, zr_plus, core_pal).wait_send()
            y_copy(j, t).wait_send()


def shards(
    images, references, shell_of_pixel, noise_power, ref_class, ref_orient, class_logw, orient_logw
):
    key = (ref_class * 8192 + ref_orient).reshape(NREF, 1)
    vmem = pl.BlockSpec(memory_space=pltpu.VMEM)
    hbm = pl.BlockSpec(memory_space=pl.ANY)
    smem = pl.BlockSpec(memory_space=pltpu.SMEM)
    dma = pltpu.SemaphoreType.DMA
    accumulators, evidence = pl.pallas_call(
        kernel,
        out_shape=(
            jax.ShapeDtypeStruct((ROWS, PIX), F32),
            jax.ShapeDtypeStruct((1, NIM), F32),
        ),
        in_specs=[hbm, hbm, vmem, vmem, vmem, vmem, smem],
        out_specs=(vmem, vmem),
        scratch_shapes=[
            pltpu.VMEM((NIM, PIX), BF16),
            pltpu.VMEM((NIM, PIX), BF16),
            pltpu.VMEM((4, GROUP, PIX), BF16),
            pltpu.VMEM((4, GROUP, NIM), F32),
            pltpu.VMEM((4, GROUP, HALF), F32),
            pltpu.VMEM((4, SIDE, HALF), F32),
            pltpu.VMEM((4, SIDE, HALF), F32),
            pltpu.VMEM((4, SIDE, HALF), F32),
            pltpu.VMEM((1, PIX), F32),
            pltpu.VMEM((4 * SIDE, 1), jnp.int32),
            pltpu.VMEM((4 * SIDE, 1), F32),
            pltpu.VMEM((24, HALF), F32),
            pltpu.VMEM((24, HALF), F32),
            pltpu.VMEM((4, GROUP, NIM), BF16),
            pltpu.VMEM((NT, GROUP, TILE), BF16),
            pltpu.VMEM((NT, GROUP, TILE), BF16),
            pltpu.VMEM((NT, GROUP, TILE), BF16),
            pltpu.VMEM((NT, GROUP, TILE), BF16),
            pltpu.VMEM((NT, GROUP, TILE), BF16),
            pltpu.VMEM((NT, GROUP, TILE), BF16),
            pltpu.VMEM((NT, GROUP, TILE), F32),
            pltpu.VMEM((NT, 2, 32, TILE), BF16),
            pltpu.VMEM((NT, 2, 32, TILE), BF16),
            pltpu.VMEM((NT, 2, 32, TILE), BF16),
            pltpu.VMEM((NT, 2, 32, TILE), BF16),
            pltpu.VMEM((NT, 2, 32, TILE), BF16),
            pltpu.VMEM((NT, 2, 32, TILE), BF16),
            pltpu.VMEM((NT, 2, PIECE, TILE), BF16),
            pltpu.VMEM((NT, 2, PIECE, TILE), BF16),
            dma((5,)),
            dma((84,)),
            dma((84,)),
            dma((24,)),
            dma((24,)),
            dma((3, NT, 2)),
            dma((3, NT, 2)),
            dma((3, NT, 2)),
            dma((3, NT, 2)),
            dma((NT, 2)),
            dma((NT, 2)),
        ],
        compiler_params=pltpu.CompilerParams(
            collective_id=0, has_side_effects=True, vmem_limit_bytes=67043328
        ),
    )(
        images,
        references,
        shell_of_pixel.reshape(1, PIX),
        noise_power.reshape(1, 64),
        key,
        orient_logw.reshape(1, NORIENT),
        class_logw,
    )
    return accumulators, evidence.reshape(NIM)


def solution(mesh):
    placed = (P("img", "shell"), P("img", "shell"), P("shell"), P(), P(), P(), P(), P())
    return jax.shard_map(
        shards, mesh=mesh, in_specs=placed, out_specs=(P("img", "shell"), P("img")), check_vma=False
    )
```

time: 502 us -> 139 us (0.28); the launches traced: 494 us -> 139 us
  waiting for transfers between devices: 389 us -> 0 us
  Pallas kernels: 0 us -> 134 us
  matrix products: 41.3 us -> 0 us
  blocking collectives: 31.6 us -> 0 us
  between operations: 14.1 us -> 0.64 us
    reduce_scatter x1 -> x0, waiting for transfers between devices: 194 us -> none  [shards(): lax.psum_scatter(lax.dot_general(posterior, images, (((0,), (0,)), ((), (...]
    all_gather x1 -> x0, waiting for transfers between devices: 162 us -> none  [shards(): reference_block_list = lax.all_gather(references, 'img', axis=0, tiled=True)]
    pallas_call x0 -> x1, Pallas kernels: none -> 134 us  [shards(): pl.pallas_call(kernel, out_shape=(jax.ShapeDtypeStruct((ROWS, PIX), F32),...]
    dot_general x3 -> x0, matrix products: 41.3 us -> none  [the longest x1 18 us: shards(): jnp.dot(block_float * block_float, weights, precision=lax.Precision.HIGHEST)]
    all_to_all x1 -> x0, waiting for transfers between devices: 32 us -> none  [sum_at_owner(): tiles = lax.all_to_all(split_up(array, dim, peers), axis, 0, 0, tiled=True)]
    all_to_all x2 -> x0, blocking collectives: 31.6 us -> none  [sent_to_all(): lax.all_to_all(jnp.broadcast_to(array[None], (peers, *array.shape)), axis...]
    gather x1 -> x0, local copies, waits for them, and re-layouts: 6.15 us -> none  [shards(): orient_logw[ref_orient]]
  transfers between devices with their start and end apart: 3 -> 0, of which waited for: 3 -> 0; matrix products, arithmetic and copies ran while one was open for 2% -> 0% of each run, Pallas kernels for 0% -> 0%
where the time goes in v1:
time: 139 us
  Pallas kernels  134 us (96%)
  local copies, waits for them, and re-layouts  2.9 us (2%)
  other arithmetic  2.01 us (1%)
    pallas_call x1, Pallas kernels, shards(): pl.pallas_call(kernel, out_shape=(jax.ShapeDtypeStruct((ROWS, PIX), F32),...  134 us

profile of v1, /device:TPU:8, one launch (start us, length us, event | category | flops | bytes accessed | tf_op | source)
XLA Modules:
  0.0 139.1 jit_solution(6817837436261691010)
XLA Ops:
  0.6 0.7 multiply_add_fusion
  1.4 1.0 copy.10.key_ref
  2.4 133.6 %shard_map.95 = (f32[32,4096]{1,0:T(8,128)}, f32[1,768]{1,0:T(1,128)}) custom-call(bf16[768,4096]{1,0:T(8,128)(2,1)} %images_hbm.1, bf16[32,4096]{1,0:T(8,128)(2,1)} %references_hbm.1, s32[1,4096]{1,0:T(1,128)} %bitcast.5, f32[1,64]{1,0:T(1,128)} %bitcast.7, s32[1024,1]{1,0:T(8,128)} %copy.10.key_ref, f32[1,6144]{1,0:T(1,128)} %bitcast.4, f32[4]{0:T(128)} %class_ref.1), custom_call_target="tpu_custom_call" | custom-call | tf_op jit(solution)/shard_map/pallas_call | solution.py:515
  135.9 1.3 reduce
  137.2 1.9 %copy.12 = f32[32,4096]{1,0:T(8,128)} copy(f32[32,4096]{1,0:T(8,128)} %get-tuple-element.8) | data formatting | bytes 1048576

commit v2 on v1

--- a/solution.py
+++ b/solution.py
@@ -30,7 +30,8 @@
     references_hbm,
     shell_ref,
     noise_ref,
-    key_ref,
+    class_id_ref,
+    orient_id_ref,
     orient_ref,
     class_ref,
     out_ref,
@@ -44,8 +45,10 @@
     row_in,
     total,
     weight,
-    keys,
+    square,
+    columns,
     prior,
+    evid,
     stat_out,
     stat_in,
     post,
@@ -164,6 +167,49 @@
         ag_send(("a+", t, b, yr), piece(t, 0, b, yr), piece(t, 3, b, yr), a_plus[t])
         ag_send(("a-", t, b, yr), piece(t, 0, b, yr), piece(t, 1, b, yr), a_minus[t])
 
+    def log_prior():
+        square[...] = jnp.zeros((128, 128), F32)
+        for n, ids in enumerate((class_id_ref, orient_id_ref)):
+            square[0:8, :] = ids[...].astype(F32)
+            columns[n] = square[...].T
+
+        def place(block, row, a, b, yr, kind):
+            za = lax.rem(z + jnp.where(kind == 0, b, a), NZ)
+            xa = lax.rem(x + jnp.where(kind == 0, a, b), NX)
+            ya = y if yr == 0 else 1 - y
+            first = at(za, ya, xa) * ROWS + kind * PIECE
+            rows = pl.ds(pl.multiple_of(lax.rem(first, 128), PIECE), PIECE)
+            pick = lax.broadcasted_iota(jnp.int32, (PIECE, 128), 1) == first // 128
+            for n in range(2):
+                found = jnp.sum(jnp.where(pick, columns[n, rows, :], 0.0), axis=1, keepdims=True)
+                prior[n, pl.ds(block * SIDE + row, PIECE), :] = found
+
+        for b in range(4):
+            for yr in range(2):
+                for g in (0, 1, 3):
+                    place(g, b * 32 + yr * PIECE, g, b, yr, y_hi)
+                for t in range(2):
+                    row = t * 64 + (b % 2) * 32 + yr * PIECE
+                    place(2 + 2 * (b // 2), row, 2, b, yr, t)
+
+        @pl.loop(0, 5)
+        def _(block):
+            rows = pl.ds(pl.multiple_of(block * SIDE, SIDE), SIDE)
+            kind = prior[0, rows, :]
+            orient = jnp.broadcast_to(prior[1, rows, :], (SIDE, 128)).astype(jnp.int32)
+
+            def add(n, sums):
+                cols = pl.ds(pl.multiple_of(n * 128, 128), 128)
+                ids = lax.broadcasted_iota(jnp.int32, (SIDE, 128), 1) + n * 128
+                logw = jnp.broadcast_to(orient_ref[:, cols], (SIDE, 128))
+                return sums + jnp.where(orient == ids, logw, 0.0)
+
+            sums = lax.fori_loop(0, NORIENT // 128, add, jnp.zeros((SIDE, 128), F32))
+            found = jnp.zeros((SIDE, 1), F32)
+            for n in range(4):
+                found = found + jnp.where(kind == float(n), class_ref[n], 0.0)
+            prior[0, rows, :] = found + jnp.sum(sums, axis=1, keepdims=True)
+
     for t in range(2):
         own[t].wait()
     for t in range(2):
@@ -213,35 +259,7 @@
             send_a(t, 3, yr)
             send_a(t, 1, yr)
         if yr == 0:
-            for a in range(4):
-                for b in range(4):
-                    for yr2 in range(2):
-                        za = lax.rem(z + jnp.where(y_hi == 0, b, a), NZ)
-                        xa = lax.rem(x + jnp.where(y_hi == 0, a, b), NX)
-                        ya = y if yr2 == 0 else 1 - y
-                        first = at(za, ya, xa) * ROWS + y_hi * PIECE
-                        keys[pl.ds(a * SIDE + b * 32 + yr2 * PIECE, PIECE), :] = key_ref[
-                            pl.ds(pl.multiple_of(first, PIECE), PIECE), :
-                        ]
-
-            @pl.loop(0, 4)
-            def _(a):
-                rows = pl.ds(pl.multiple_of(a * SIDE, SIDE), SIDE)
-                key = keys[rows, :]
-                orient = jnp.broadcast_to(lax.rem(key, 8192), (SIDE, 128))
-                kind = key // 8192
-
-                def add(n, sums):
-                    cols = pl.ds(pl.multiple_of(n * 128, 128), 128)
-                    ids = lax.broadcasted_iota(jnp.int32, (SIDE, 128), 1) + n * 128
-                    logw = jnp.broadcast_to(orient_ref[:, cols], (SIDE, 128))
-                    return sums + jnp.where(orient == ids, logw, 0.0)
-
-                sums = lax.fori_loop(0, NORIENT // 128, add, jnp.zeros((SIDE, 128), F32))
-                found = jnp.zeros((SIDE, 1), F32)
-                for n in range(4):
-                    found = found + jnp.where(kind == n, class_ref[n], 0.0)
-                prior[rows, :] = found + jnp.sum(sums, axis=1, keepdims=True)
+            log_prior()
 
     for yr in range(2):
         for t in range(2):
@@ -263,23 +281,25 @@
     def ex_wait(n, dst):
         landed(dst, ex_s.at[n], ex_r.at[n])
 
-    def do_scores(g):
+    def scores(r, out, n_rows):
         def add(n, sums):
             cols = pl.ds(pl.multiple_of(n * 128, 128), 128)
-            r = refs[g, :, cols].astype(F32)
-            return sums + r * r * weight[:, cols]
-
-        sums = lax.fori_loop(0, PIX // 128, add, jnp.zeros((GROUP, 128), F32))
+            part = r(cols).astype(F32)
+            return sums + part * part * weight[:, cols]
+
+        sums = lax.fori_loop(0, PIX // 128, add, jnp.zeros((n_rows, 128), F32))
         norm = 0.5 * jnp.sum(sums, axis=1, keepdims=True)
 
         @pl.loop(0, 3)
         def _(n):
             rows = pl.ds(pl.multiple_of(n * 256, 256), 256)
             part = lax.dot_general(
-                refs[g], wim[rows, :], (((1,), (1,)), ((), ())), preferred_element_type=F32
+                r(slice(None)), wim[rows, :], (((1,), (1,)), ((), ())), preferred_element_type=F32
             )
-            score[g, :, rows] = part - norm
-
+            out[:, rows] = part - norm
+
+    def do_scores(g):
+        scores(lambda cols: refs[g, :, cols], score.at[g], GROUP)
         ex_send(g, score.at[g, :, theirs], core_in.at[g], core_pal)
 
     def do_rows(g):
@@ -288,57 +308,106 @@
         ex_send(4 + g, row_out.at[g], row_in.at[g], hi_pal)
         total[g] = score[g, keep, mine] + core_in[g, keep, :]
 
-    def do_logits(g):
-        ex_wait(4 + g, row_in.at[g])
-        rows = pl.ds(g * SIDE, SIDE)
-        logits = INVERSE_HEAT * (total[g] + row_in[g]) + prior[rows, :]
-        total[g] = logits
+    half_rows = (pl.ds(0, SIDE), pl.ds(SIDE, SIDE))
+
+    def do_scores_2(h):
+        def r(cols):
+            low = refs[2, h * 64 : h * 64 + 64, cols]
+            return jnp.concatenate([low, refs[2, SIDE + h * 64 : SIDE + h * 64 + 64, cols]], axis=0)
+
+        scores(r, score.at[2, half_rows[h]], SIDE)
+        n = (2, 10)[h]
+        ex_send(n, score.at[2, half_rows[h], theirs], core_in.at[2, half_rows[h]], core_pal)
+
+    def do_rows_2(h):
+        ex_wait((2, 10)[h], core_in.at[2, half_rows[h]])
+        block = 2 + 2 * h
+        row_out[block] = score[2, half_rows[h], mine] + core_in[2, half_rows[h], :]
+        ex_send((6, 11)[h], row_out.at[block], row_in.at[block], hi_pal)
+
+    def do_logits(block):
+        rows = pl.ds(block * SIDE, SIDE)
+        if block in (2, 4):
+            ex_wait({2: 6, 4: 11}[block], row_in.at[block])
+            summed = row_out[block] + row_in[block]
+        else:
+            ex_wait(4 + block, row_in.at[block])
+            summed = total[block] + row_in[block]
+        logits = INVERSE_HEAT * summed + prior[0, rows, :]
+        total[block] = logits
         return jnp.max(logits, axis=0, keepdims=True)
+
+    def mass_of(blocks, top):
+        mass = jnp.zeros((1, HALF), F32)
+        for block in blocks:
+            mass = mass + jnp.sum(jnp.exp(total[block] - top), axis=0, keepdims=True)
+        return mass
 
     do_scores(0)
     order = [(0, 0), (0, 1), (3, 0), (1, 0), (3, 1), (1, 1), (2, 0), (2, 1)]
+    forward = [(0, 0), (0, 1), (1, 0), (1, 1), (3, 0), (3, 1), (2, 0), (2, 1)]
+    arrived = []
+    passed = 0
     for n, (b, yr) in enumerate(order):
         for t in range(2):
             ag_wait(("a+", t, b, yr), piece(t, 3, b, yr))
-            ag_send(("af+", t, b, yr), piece(t, 3, b, yr, 0), piece(t, 2, b, yr, 0), a_plus[t])
             ag_wait(("a-", t, b, yr), piece(t, 1, b, yr))
-            ag_send(("af-", t, b, yr), piece(t, 1, b, yr, 1), piece(t, 2, b, yr, 1), a_minus[t])
+        arrived.append((b, yr))
+        while passed < 8 and forward[passed] in arrived:
+            b, yr = forward[passed]
+            for t in range(2):
+                ag_send(("af+", t, b, yr), piece(t, 3, b, yr, 0), piece(t, 2, b, yr, 0), a_plus[t])
+                ag_send(("af-", t, b, yr), piece(t, 1, b, yr, 1), piece(t, 2, b, yr, 1), a_minus[t])
+            passed += 1
         if n == 1:
             do_rows(0)
     do_scores(1)
     do_scores(3)
     do_rows(1)
     do_rows(3)
-    for b, yr in order:
-        for t in range(2):
-            ag_wait(("af+", t, b, yr), piece(t, 2, b, yr, 0))
-            ag_wait(("af-", t, b, yr), piece(t, 2, b, yr, 1))
-    do_scores(2)
+
+    def opposite_landed(pieces):
+        for b, yr in pieces:
+            for t in range(2):
+                ag_wait(("af+", t, b, yr), piece(t, 2, b, yr, 0))
+                ag_wait(("af-", t, b, yr), piece(t, 2, b, yr, 1))
+
+    opposite_landed(forward[:4])
+    do_scores_2(0)
     top = do_logits(0)
+    do_rows_2(0)
+    opposite_landed(forward[4:])
+    do_scores_2(1)
     top = jnp.maximum(top, do_logits(1))
-    do_rows(2)
     top = jnp.maximum(top, do_logits(3))
-    top = jnp.maximum(top, do_logits(2))
-    mass = jnp.zeros((1, HALF), F32)
-    for g in range(4):
-        mass = mass + jnp.sum(jnp.exp(total[g] - top), axis=0, keepdims=True)
-    stat_out[0:8, :] = jnp.broadcast_to(top, (8, HALF))
-    stat_out[8:16, :] = jnp.broadcast_to(mass, (8, HALF))
-    ex_send(8, stat_out.at[0:16], stat_in.at[0:16], hi_pal)
-    ex_wait(8, stat_in.at[0:16])
-    other_top, other_mass = stat_in[0:1, :], stat_in[8:9, :]
+    mass = mass_of((0, 1, 3), top)
+    stat_out[0:1, :] = top
+    stat_out[1:2, :] = mass
+    do_rows_2(1)
+    ex_send(8, stat_out.at[0:8], stat_in.at[0:8], hi_pal)
+    last_top = do_logits(2)
+    ex_wait(8, stat_in.at[0:8])
+    other_top, other_mass = stat_in[0:1, :], stat_in[1:2, :]
     first = y_hi == 0
     top_a, top_b = jnp.where(first, top, other_top), jnp.where(first, other_top, top)
     mass_a, mass_b = jnp.where(first, mass, other_mass), jnp.where(first, other_mass, mass)
-    best = jnp.maximum(top_a, top_b)
-    evidence = best + jnp.log(mass_a * jnp.exp(top_a - best) + mass_b * jnp.exp(top_b - best))
-    stat_out[16:24, :] = jnp.broadcast_to(evidence, (8, HALF))
-    gs = (2, 1, 3, 0)
-    for g in gs:
+    last_top = jnp.maximum(last_top, do_logits(4))
+    best = jnp.maximum(jnp.maximum(top_a, top_b), last_top)
+    evidence = best + jnp.log(
+        mass_a * jnp.exp(top_a - best) + mass_b * jnp.exp(top_b - best) + mass_of((2, 4), best)
+    )
+    for h in range(2):
+        p = jnp.exp(total[2 + 2 * h] - evidence).astype(BF16)
+        for t in range(2):
+            rows = pl.ds(t * SIDE + h * 64, 64)
+            post[2, rows, mine] = p[t * 64 : t * 64 + 64, :]
+    ex_send(18, post.at[2, :, mine], post.at[2, :, mine], core_pal)
+    stat_out[8:16, :] = jnp.broadcast_to(evidence, (8, HALF))
+    for g in (1, 3, 0):
         post[g, keep, mine] = jnp.exp(total[g] - evidence).astype(BF16)
         ex_send(12 + g, post.at[g, keep, mine], post.at[g, keep, mine], hi_pal)
         ex_send(16 + g, post.at[g, keep, mine], post.at[g, keep, mine], core_pal)
-    ex_send(9, stat_out.at[16:24], stat_in.at[16:24], core_pal)
+    ex_send(9, stat_out.at[8:16], stat_in.at[8:16], core_pal)
 
     def do_relay(g):
         ex_wait(12 + g, post.at[g, give, mine])
@@ -363,9 +432,7 @@
     def a_landed(kind, j, t, dst):
         landed(dst.at[j, half(t)], a_s.at[kind, j, t], a_r.at[kind, j, t])
 
-    do_relay(2)
-    do_posterior(2)
-    do_relay(1)
+    ex_wait(18, post.at[2, :, theirs])
 
     @pl.loop(0, 4)
     def _(k):
@@ -376,6 +443,7 @@
         for t in range(2):
             a_copy(0, k + 4, t, s2, r_opp, a_minus[t]).start()
 
+    do_relay(1)
     do_relay(3)
     do_posterior(1)
     do_posterior(3)
@@ -391,9 +459,11 @@
             a_copy(2, k, t, s3, r_plus, a_minus[t]).start()
 
     do_posterior(0)
-    ex_wait(9, stat_in.at[16:24])
-    evidence_ref[:, mine] = stat_out[16:17, :]
-    evidence_ref[:, theirs] = stat_in[16:17, :]
+    ex_wait(9, stat_in.at[8:16])
+    evid[:, mine] = stat_out[8:9, :]
+    evid[:, theirs] = stat_in[8:9, :]
+    for n in range(NIM // 128):
+        evidence_ref[n : n + 1, :] = evid[:, n * 128 : n * 128 + 128]
 
     @pl.loop(0, 4)
     def _(k):
@@ -507,7 +577,6 @@
 def shards(
     images, references, shell_of_pixel, noise_power, ref_class, ref_orient, class_logw, orient_logw
 ):
-    key = (ref_class * 8192 + ref_orient).reshape(NREF, 1)
     vmem = pl.BlockSpec(memory_space=pltpu.VMEM)
     hbm = pl.BlockSpec(memory_space=pl.ANY)
     smem = pl.BlockSpec(memory_space=pltpu.SMEM)
@@ -516,9 +585,9 @@
         kernel,
         out_shape=(
             jax.ShapeDtypeStruct((ROWS, PIX), F32),
-            jax.ShapeDtypeStruct((1, NIM), F32),
+            jax.ShapeDtypeStruct((NIM // 128, 128), F32),
         ),
-        in_specs=[hbm, hbm, vmem, vmem, vmem, vmem, smem],
+        in_specs=[hbm, hbm, vmem, vmem, vmem, vmem, vmem, smem],
         out_specs=(vmem, vmem),
         scratch_shapes=[
             pltpu.VMEM((NIM, PIX), BF16),
@@ -526,14 +595,16 @@
             pltpu.VMEM((4, GROUP, PIX), BF16),
             pltpu.VMEM((4, GROUP, NIM), F32),
             pltpu.VMEM((4, GROUP, HALF), F32),
-            pltpu.VMEM((4, SIDE, HALF), F32),
-            pltpu.VMEM((4, SIDE, HALF), F32),
-            pltpu.VMEM((4, SIDE, HALF), F32),
+            pltpu.VMEM((5, SIDE, HALF), F32),
+            pltpu.VMEM((5, SIDE, HALF), F32),
+            pltpu.VMEM((5, SIDE, HALF), F32),
             pltpu.VMEM((1, PIX), F32),
-            pltpu.VMEM((4 * SIDE, 1), jnp.int32),
-            pltpu.VMEM((4 * SIDE, 1), F32),
-            pltpu.VMEM((24, HALF), F32),
-            pltpu.VMEM((24, HALF), F32),
+            pltpu.VMEM((128, 128), F32),
+            pltpu.VMEM((2, 128, 128), F32),
+            pltpu.VMEM((2, 5 * SIDE, 1), F32),
+            pltpu.VMEM((1, NIM), F32),
+            pltpu.VMEM((16, HALF), F32),
+            pltpu.VMEM((16, HALF), F32),
             pltpu.VMEM((4, GROUP, NIM), BF16),
             pltpu.VMEM((NT, GROUP, TILE), BF16),
             pltpu.VMEM((NT, GROUP, TILE), BF16),
@@ -570,7 +641,8 @@
         references,
         shell_of_pixel.reshape(1, PIX),
         noise_power.reshape(1, 64),
-        key,
+        ref_class.reshape(NREF // 128, 128),
+        ref_orient.reshape(NREF // 128, 128),
         orient_logw.reshape(1, NORIENT),
         class_logw,
     )

time: 139 us -> 131 us (0.942)
  Pallas kernels: 134 us -> 127 us
  other arithmetic: 2.01 us -> 0 us
    pallas_call x1, Pallas kernels: 134 us -> 127 us  [shards(): pl.pallas_call(kernel, out_shape=(jax.ShapeDtypeStruct((ROWS, PIX), F32),...]
    unnamed x1 -> x2, local copies, waits for them, and re-layouts: 1.87 us -> 3.14 us
where the time goes in v2:
time: 131 us
  Pallas kernels  127 us (97%)
  local copies, waits for them, and re-layouts  3.14 us (2%)
    pallas_call x1, Pallas kernels, shards(): pl.pallas_call(kernel, out_shape=(jax.ShapeDtypeStruct((ROWS, PIX), F32),...  127 us
    unnamed x2, local copies, waits for them, and re-layouts  3.14 us

profile of v2, /device:TPU:8, one launch (start us, length us, event | category | flops | bytes accessed | tf_op | source)
XLA Modules:
  0.0 130.7 jit_solution(14863135993029900930)
XLA Ops:
  0.6 126.9 %shard_map.95 = (f32[32,4096]{1,0:T(8,128)}, f32[6,128]{1,0:T(8,128)}) custom-call(bf16[768,4096]{1,0:T(8,128)(2,1)} %images_hbm.1, bf16[32,4096]{1,0:T(8,128)(2,1)} %references_hbm.1, s32[1,4096]{1,0:T(1,128)} %bitcast.7, f32[1,64]{1,0:T(1,128)} %bitcast.11, s32[8,128]{1,0:T(8,128)} %bitcast.9, s32[8,128]{1,0:T(8,128)} %bitcast.10, f32[1,6144]{1,0:T(1,128)} %bitcast.6, ...), custom_call_target="tpu_custom_call" | custom-call | tf_op jit(solution)/shard_map/pallas_call | solution.py:584
  127.5 1.9 %copy.12 = f32[32,4096]{1,0:T(8,128)} copy(f32[32,4096]{1,0:T(8,128)} %get-tuple-element.8) | data formatting | bytes 1048576
  129.4 1.3 copy.13

commit v3 on v2

--- a/solution.py
+++ b/solution.py
@@ -67,6 +67,9 @@
     zr_minus,
     y_out,
     y_in,
+    kept,
+    f_out,
+    f_in,
     load_sem,
     ag_s,
     ag_r,
@@ -78,6 +81,8 @@
     b_r,
     yy_s,
     yy_r,
+    f_s,
+    f_r,
 ):
     s = lax.axis_index("shell")
     i = lax.axis_index("img")
@@ -421,20 +426,41 @@
         cols = pl.ds(pl.multiple_of(j * TILE, TILE), TILE)
         return jnp.dot(post[g], im[:, cols], preferred_element_type=F32)
 
-    def half(t):
-        return pl.ds(t * SIDE, SIDE)
+    def a_rows(j, t):
+        return pl.ds(t * SIDE, 64 if isinstance(j, int) and j % 4 == 3 else SIDE)
 
     def a_copy(kind, j, t, src, dst, peer):
+        rows = a_rows(j, t)
         return remote(
-            src.at[j, half(t)], dst.at[j, half(t)], a_s.at[kind, j, t], a_r.at[kind, j, t], peer
+            src.at[j, rows], dst.at[j, rows], a_s.at[kind, j, t], a_r.at[kind, j, t], peer
         )
 
     def a_landed(kind, j, t, dst):
-        landed(dst.at[j, half(t)], a_s.at[kind, j, t], a_r.at[kind, j, t])
+        landed(dst.at[j, a_rows(j, t)], a_s.at[kind, j, t], a_r.at[kind, j, t])
+
+    def f_copy(g, n):
+        return remote(f_out.at[n, g], f_in.at[n, g], f_s.at[n, g], f_r.at[n, g], y_pal)
+
+    def first_product(g, n):
+        p = product(g, 3 + 4 * n).reshape(8, 2, PIECE, TILE)
+        f_out[n, g] = p[:, 1].reshape(SIDE, TILE).astype(BF16)
+        f_copy(g, n).start()
+        kept[n, g] = p[:, 0].reshape(SIDE, TILE)
+
+    def first_sum(g, n):
+        f_copy(g, n).wait_recv()
+        return kept[n, g] + f_in[n, g].astype(F32)
+
+    def put(dst, j, rows):
+        for t in range(2):
+            dst[j, a_rows(j, t)] = rows[t * 64 : t * 64 + 64, :].astype(BF16)
+
+    def get(src, j):
+        return jnp.concatenate([src[j, a_rows(j, t)] for t in range(2)], axis=0).astype(F32)
 
     ex_wait(18, post.at[2, :, theirs])
 
-    @pl.loop(0, 4)
+    @pl.loop(0, 3)
     def _(k):
         s2[k] = product(2, k).astype(BF16)
         for t in range(2):
@@ -443,13 +469,14 @@
         for t in range(2):
             a_copy(0, k + 4, t, s2, r_opp, a_minus[t]).start()
 
+    for n in range(2):
+        first_product(2, n)
     do_relay(1)
     do_relay(3)
     do_posterior(1)
     do_posterior(3)
-    do_relay(0)
-
-    @pl.loop(0, 4)
+
+    @pl.loop(0, 3)
     def _(k):
         s1[k + 4] = product(1, k + 4).astype(BF16)
         for t in range(2):
@@ -458,112 +485,160 @@
         for t in range(2):
             a_copy(2, k, t, s3, r_plus, a_minus[t]).start()
 
+    first_product(1, 1)
+    first_product(3, 0)
+    first_product(1, 0)
+    first_product(3, 1)
+    do_relay(0)
     do_posterior(0)
+    for n in range(2):
+        first_product(0, n)
+
+    @pl.loop(0, 3)
+    def _(k):
+        p1 = product(1, k)
+        for t in range(2):
+            a_landed(0, k, t, r_opp)
+        s1[k] = (p1 + r_opp[k].astype(F32)).astype(BF16)
+        for t in range(2):
+            a_copy(1, k, t, s1, r_minus, a_plus[t]).start()
+        p3 = product(3, k + 4)
+        for t in range(2):
+            a_landed(0, k + 4, t, r_opp)
+        s3[k + 4] = (p3 + r_opp[k + 4].astype(F32)).astype(BF16)
+        for t in range(2):
+            a_copy(2, k + 4, t, s3, r_plus, a_minus[t]).start()
+
     ex_wait(9, stat_in.at[8:16])
     evid[:, mine] = stat_out[8:9, :]
     evid[:, theirs] = stat_in[8:9, :]
     for n in range(NIM // 128):
         evidence_ref[n : n + 1, :] = evid[:, n * 128 : n * 128 + 128]
 
-    @pl.loop(0, 4)
-    def _(k):
-        p1 = product(1, k)
-        for t in range(2):
-            a_landed(0, k, t, r_opp)
-        s1[k] = (p1 + r_opp[k].astype(F32)).astype(BF16)
-        for t in range(2):
-            a_copy(1, k, t, s1, r_minus, a_plus[t]).start()
-        p3 = product(3, k + 4)
-        for t in range(2):
-            a_landed(0, k + 4, t, r_opp)
-        s3[k + 4] = (p3 + r_opp[k + 4].astype(F32)).astype(BF16)
-        for t in range(2):
-            a_copy(2, k + 4, t, s3, r_plus, a_minus[t]).start()
-
     def b_copy(kind, j, t, src, dst, peer):
-        return remote(src.at[j, t], dst.at[j, t], b_s.at[kind, j, t], b_r.at[kind, j, t], peer)
+        rows = pl.ds(0, PIECE if j % 4 == 3 else 32)
+        return remote(
+            src.at[j, t, rows], dst.at[j, t, rows], b_s.at[kind, j, t], b_r.at[kind, j, t], peer
+        )
 
     def b_landed(kind, j, t, dst):
-        landed(dst.at[j, t], b_s.at[kind, j, t], b_r.at[kind, j, t])
+        b_copy(kind, j, t, dst, dst, core_pal).wait_recv()
 
     def y_copy(j, t):
         return remote(y_out.at[j, t], y_in.at[j, t], yy_s.at[j, t], yy_r.at[j, t], y_pal)
 
+    def first_opposite():
+        for n, j in enumerate((3, 7)):
+            put(s2, j, first_sum(2, n))
+            for t in range(2):
+                a_copy(0, j, t, s2, r_opp, (a_plus, a_minus)[n][t]).start()
+
+    def first_free():
+        put(s1, 7, first_sum(1, 1))
+        for t in range(2):
+            a_copy(1, 7, t, s1, r_minus, a_plus[t]).start()
+        put(s3, 3, first_sum(3, 0))
+        for t in range(2):
+            a_copy(2, 3, t, s3, r_plus, a_minus[t]).start()
+
+    def first_bound():
+        for t in range(2):
+            a_landed(0, 3, t, r_opp)
+        put(s1, 3, first_sum(1, 0) + get(r_opp, 3))
+        for t in range(2):
+            a_copy(1, 3, t, s1, r_minus, a_plus[t]).start()
+        for t in range(2):
+            a_landed(0, 7, t, r_opp)
+        put(s3, 7, first_sum(3, 1) + get(r_opp, 7))
+        for t in range(2):
+            a_copy(2, 7, t, s3, r_plus, a_minus[t]).start()
+
+    def rows_of(j, t, b):
+        n = PIECE if j % 4 == 3 else 32
+        return pl.ds(t * SIDE + b * n, n)
+
     def step_a(k):
         for j, low in ((k, True), (k + 4, False)):
-            p = product(0, j)
+            p = None if k == 3 else product(0, j)
             for t in range(2):
                 a_landed(1, j, t, r_minus)
                 a_landed(2, j, t, r_plus)
-            acc[j] = p + r_plus[j].astype(F32) + r_minus[j].astype(F32)
+            if k == 3:
+                total_j = first_sum(0, j // 4) + get(r_plus, j) + get(r_minus, j)
+                for t in range(2):
+                    acc[j, a_rows(j, t)] = total_j[t * 64 : t * 64 + 64, :]
+            else:
+                acc[j] = p + r_plus[j].astype(F32) + r_minus[j].astype(F32)
+            n = PIECE if k == 3 else 32
             for t in range(2):
-                o = t * SIDE
-                z2[j, t] = acc[j, o + 64 : o + 96, :].astype(BF16)
+                z2[j, t, 0:n] = acc[j, rows_of(j, t, 2), :].astype(BF16)
                 b_copy(0, j, t, z2, zr_opp, b_plus[t] if low else b_minus[t]).start()
                 if low:
-                    z3[j, t] = acc[j, o + 96 : o + 128, :].astype(BF16)
+                    z3[j, t, 0:n] = acc[j, rows_of(j, t, 3), :].astype(BF16)
                     b_copy(2, j, t, z3, zr_plus, b_minus[t]).start()
                 else:
-                    z1[j, t] = acc[j, o + 32 : o + 64, :].astype(BF16)
+                    z1[j, t, 0:n] = acc[j, rows_of(j, t, 1), :].astype(BF16)
                     b_copy(1, j, t, z1, zr_minus, b_plus[t]).start()
 
     def step_b(k):
-        for t in range(2):
-            o = t * SIDE
+        n = PIECE if k == 3 else 32
+        for t in range(2):
             b_landed(0, k, t, zr_opp)
-            z1[k, t] = (acc[k, o + 32 : o + 64, :] + zr_opp[k, t].astype(F32)).astype(BF16)
+            v = acc[k, rows_of(k, t, 1), :] + zr_opp[k, t, 0:n].astype(F32)
+            z1[k, t, 0:n] = v.astype(BF16)
             b_copy(1, k, t, z1, zr_minus, b_plus[t]).start()
             j = k + 4
             b_landed(0, j, t, zr_opp)
-            z3[j, t] = (acc[j, o + 96 : o + 128, :] + zr_opp[j, t].astype(F32)).astype(BF16)
+            v = acc[j, rows_of(j, t, 3), :] + zr_opp[j, t, 0:n].astype(F32)
+            z3[j, t, 0:n] = v.astype(BF16)
             b_copy(2, j, t, z3, zr_plus, b_minus[t]).start()
 
     def step_c(k):
+        n = PIECE if k == 3 else 32
         for j in (k, k + 4):
+            cols = pl.ds(j * TILE, TILE)
             for t in range(2):
-                o = t * SIDE
                 b_landed(1, j, t, zr_minus)
                 b_landed(2, j, t, zr_plus)
-                v = acc[j, o : o + 32, :] + zr_plus[j, t].astype(F32) + zr_minus[j, t].astype(F32)
-                y_out[j, t] = v[PIECE:, :].astype(BF16)
-                y_copy(j, t).start()
-                acc[j, o : o + PIECE, :] = v[:PIECE, :]
+                v = acc[j, rows_of(j, t, 0), :] + zr_plus[j, t, 0:n].astype(F32)
+                v = v + zr_minus[j, t, 0:n].astype(F32)
+                out_ref[t * PIECE : (t + 1) * PIECE, cols] = v[:PIECE, :]
+                if k < 3:
+                    y_out[j, t] = v[PIECE:, :].astype(BF16)
+                    y_copy(j, t).start()
 
     def step_d(k):
         for j in (k, k + 4):
+            cols = pl.ds(j * TILE, TILE)
             for t in range(2):
-                o = t * SIDE
                 y_copy(j, t).wait_recv()
-                cols = pl.ds(pl.multiple_of(j * TILE, TILE), TILE)
-                out_ref[t * PIECE : (t + 1) * PIECE, cols] = acc[j, o : o + PIECE, :] + y_in[
-                    j, t
-                ].astype(F32)
-
-    @pl.loop(0, 7)
-    def _(k):
-        @pl.when(k < 4)
-        def _():
-            step_a(k)
-
-        @pl.when(jnp.logical_and(k >= 1, k < 5))
-        def _():
-            step_b(k - 1)
-
-        @pl.when(jnp.logical_and(k >= 2, k < 6))
-        def _():
-            step_c(k - 2)
-
-        @pl.when(k >= 3)
-        def _():
-            step_d(k - 3)
+                rows = slice(t * PIECE, (t + 1) * PIECE)
+                out_ref[rows, cols] = out_ref[rows, cols] + y_in[j, t].astype(F32)
+
+    first_opposite()
+    step_a(0)
+    first_free()
+    step_a(1)
+    step_b(0)
+    first_bound()
+    step_a(2)
+    step_b(1)
+    step_a(3)
+    step_b(2)
+    step_c(0)
+    step_b(3)
+    step_c(1)
+    step_c(2)
+    step_c(3)
+    for k in range(3):
+        step_d(k)
 
     for c in ag_sends:
         c.wait_send()
     for c in ex_sends:
         c.wait_send()
 
-    @pl.loop(0, NT)
-    def _(j):
+    for j in range(NT):
         for t in range(2):
             a_copy(0, j, t, s2, r_opp, core_pal).wait_send()
             a_copy(1, j, t, s1, r_minus, core_pal).wait_send()
@@ -571,7 +646,11 @@
             b_copy(0, j, t, z2, zr_opp, core_pal).wait_send()
             b_copy(1, j, t, z1, zr_minus, core_pal).wait_send()
             b_copy(2, j, t, z3, zr_plus, core_pal).wait_send()
-            y_copy(j, t).wait_send()
+            if j % 4 < 3:
+                y_copy(j, t).wait_send()
+    for n in range(2):
+        for g in range(4):
+            f_copy(g, n).wait_send()
 
 
 def shards(
@@ -621,6 +700,9 @@
             pltpu.VMEM((NT, 2, 32, TILE), BF16),
             pltpu.VMEM((NT, 2, PIECE, TILE), BF16),
             pltpu.VMEM((NT, 2, PIECE, TILE), BF16),
+            pltpu.VMEM((2, 4, SIDE, TILE), F32),
+            pltpu.VMEM((2, 4, SIDE, TILE), BF16),
+            pltpu.VMEM((2, 4, SIDE, TILE), BF16),
             dma((5,)),
             dma((84,)),
             dma((84,)),
@@ -632,6 +714,8 @@
             dma((3, NT, 2)),
             dma((NT, 2)),
             dma((NT, 2)),
+            dma((2, 4)),
+            dma((2, 4)),
         ],
         compiler_params=pltpu.CompilerParams(
             collective_id=0, has_side_effects=True, vmem_limit_bytes=67043328

time: 131 us -> 123 us (0.939)
  Pallas kernels: 127 us -> 119 us
    pallas_call x1, Pallas kernels: 127 us -> 119 us  [shards(): pl.pallas_call(kernel, out_shape=(jax.ShapeDtypeStruct((ROWS, PIX), F32),...]
where the time goes in v3:
time: 123 us; the launch traced here: 122 us
  Pallas kernels  119 us (97%)
  local copies, waits for them, and re-layouts  3.14 us (3%)
    pallas_call x1, Pallas kernels, shards(): pl.pallas_call(kernel, out_shape=(jax.ShapeDtypeStruct((ROWS, PIX), F32),...  119 us
    unnamed x2, local copies, waits for them, and re-layouts  3.14 us

profile of v3, /device:TPU:8, one launch (start us, length us, event | category | flops | bytes accessed | tf_op | source)
XLA Modules:
  0.0 122.4 jit_solution(16521991365342253293)
XLA Ops:
  0.6 118.6 %shard_map.95 = (f32[32,4096]{1,0:T(8,128)}, f32[6,128]{1,0:T(8,128)}) custom-call(bf16[768,4096]{1,0:T(8,128)(2,1)} %images_hbm.1, bf16[32,4096]{1,0:T(8,128)(2,1)} %references_hbm.1, s32[1,4096]{1,0:T(1,128)} %bitcast.7, f32[1,64]{1,0:T(1,128)} %bitcast.11, s32[8,128]{1,0:T(8,128)} %bitcast.9, s32[8,128]{1,0:T(8,128)} %bitcast.10, f32[1,6144]{1,0:T(1,128)} %bitcast.6, ...), custom_call_target="tpu_custom_call" | custom-call | tf_op jit(solution)/shard_map/pallas_call | solution.py:663
  119.2 1.9 %copy.12 = f32[32,4096]{1,0:T(8,128)} copy(f32[32,4096]{1,0:T(8,128)} %get-tuple-element.8) | data formatting | bytes 1048576
  121.1 1.3 %copy.13 = f32[768]{0:T(1024)} copy(f32[768]{0:T(1024)} %bitcast.8) | data formatting | bytes 6144

commit v4 on v3

--- a/solution.py
+++ b/solution.py
@@ -23,6 +23,17 @@
 NT = PIX // TILE
 PH = PIX // 2
 NORIENT = 6144
+
+FORWARD = [(0, 0), (0, 1), (3, 0), (1, 0), (3, 1), (1, 1), (2, 0), (2, 1)]
+BATCHES = [
+    [(0, b, yr) for b, yr in FORWARD],
+    [(g, b, yr) for g in (1, 3) for b, yr in FORWARD[:4]],
+    [(g, b, yr) for g in (1, 3) for b, yr in FORWARD[4:]],
+    [(2, b, yr) for b, yr in FORWARD[:4]],
+    [(2, b, yr) for b, yr in FORWARD[4:6]],
+    [(2, b, yr) for b, yr in FORWARD[6:]],
+]
+FIRST = [0, SIDE, 2 * SIDE, 3 * SIDE, 4 * SIDE, 4 * SIDE + 64]
 
 
 def kernel(
@@ -178,7 +189,7 @@
             square[0:8, :] = ids[...].astype(F32)
             columns[n] = square[...].T
 
-        def place(block, row, a, b, yr, kind):
+        def place(row, a, b, yr, kind):
             za = lax.rem(z + jnp.where(kind == 0, b, a), NZ)
             xa = lax.rem(x + jnp.where(kind == 0, a, b), NX)
             ya = y if yr == 0 else 1 - y
@@ -187,15 +198,15 @@
             pick = lax.broadcasted_iota(jnp.int32, (PIECE, 128), 1) == first // 128
             for n in range(2):
                 found = jnp.sum(jnp.where(pick, columns[n, rows, :], 0.0), axis=1, keepdims=True)
-                prior[n, pl.ds(block * SIDE + row, PIECE), :] = found
-
-        for b in range(4):
-            for yr in range(2):
-                for g in (0, 1, 3):
-                    place(g, b * 32 + yr * PIECE, g, b, yr, y_hi)
-                for t in range(2):
-                    row = t * 64 + (b % 2) * 32 + yr * PIECE
-                    place(2 + 2 * (b // 2), row, 2, b, yr, t)
+                prior[n, pl.ds(row, PIECE), :] = found
+
+        for n, batch in enumerate(BATCHES):
+            for k, (g, b, yr) in enumerate(batch):
+                if n < 3:
+                    place(FIRST[n] + k * PIECE, g, b, yr, y_hi)
+                else:
+                    for t in range(2):
+                        place(FIRST[n] + (t * len(batch) + k) * PIECE, g, b, yr, t)
 
         @pl.loop(0, 5)
         def _(block):
@@ -254,7 +265,7 @@
             rows = pl.ds(pl.multiple_of(k * 16, 16), 16)
             wim[rows, :] = (im[rows, :].astype(F32) * weight[...]).astype(BF16)
 
-    for yr in range(2):
+    def pass_b(yr):
         for t in range(2):
             ag_wait(("b+", t, yr), piece(t, 0, 3, yr))
             ag_send(("bf+", t, yr), piece(t, 0, 3, yr, 0), piece(t, 0, 2, yr, 0), b_plus[t])
@@ -263,9 +274,27 @@
         for t in range(2):
             send_a(t, 3, yr)
             send_a(t, 1, yr)
-        if yr == 0:
-            log_prior()
-
+
+    def pass_a(b, yr):
+        for t in range(2):
+            ag_wait(("a+", t, b, yr), piece(t, 3, b, yr))
+            ag_send(("af+", t, b, yr), piece(t, 3, b, yr, 0), piece(t, 2, b, yr, 0), a_plus[t])
+            ag_wait(("a-", t, b, yr), piece(t, 1, b, yr))
+            ag_send(("af-", t, b, yr), piece(t, 1, b, yr, 1), piece(t, 2, b, yr, 1), a_minus[t])
+
+    def opposite_landed(pieces):
+        for b, yr in pieces:
+            for t in range(2):
+                ag_wait(("af+", t, b, yr), piece(t, 2, b, yr, 0))
+                ag_wait(("af-", t, b, yr), piece(t, 2, b, yr, 1))
+
+    pass_b(0)
+    log_prior()
+    pass_a(0, 0)
+    pass_a(0, 1)
+    pass_b(1)
+    pass_a(3, 0)
+    pass_a(1, 0)
     for yr in range(2):
         for t in range(2):
             ag_wait(("bf+", t, yr), piece(t, 0, 2, yr, 0))
@@ -286,60 +315,64 @@
     def ex_wait(n, dst):
         landed(dst, ex_s.at[n], ex_r.at[n])
 
-    def scores(r, out, n_rows):
-        def add(n, sums):
-            cols = pl.ds(pl.multiple_of(n * 128, 128), 128)
-            part = r(cols).astype(F32)
-            return sums + part * part * weight[:, cols]
-
-        sums = lax.fori_loop(0, PIX // 128, add, jnp.zeros((n_rows, 128), F32))
+    def places(n):
+        rows = 2 * PIECE * len(BATCHES[n])
+        return (n, pl.ds(0, rows)) if n < 3 else (3, pl.ds(FIRST[n] - FIRST[3], rows))
+
+    def sums_place(n):
+        rows = SIDE if n < 3 else 2 * PIECE * len(BATCHES[n])
+        return (FIRST[n] // SIDE, pl.ds(FIRST[n] % SIDE, rows))
+
+    def do_scores(n):
+        batch = BATCHES[n]
+        n_rows = 2 * PIECE * len(batch)
+        slot_n, rows = places(n)
+
+        def of(cols):
+            return jnp.concatenate(
+                [
+                    refs[g, t * SIDE + b * 32 + yr * PIECE : t * SIDE + b * 32 + (yr + 1) * PIECE, cols]
+                    for t in range(2)
+                    for g, b, yr in batch
+                ],
+                axis=0,
+            )
+
+        def add(k, sums):
+            for u in range(4):
+                cols = pl.ds(pl.multiple_of(k * 512 + u * 128, 128), 128)
+                part = of(cols).astype(F32)
+                sums = sums + part * part * weight[:, cols]
+            return sums
+
+        sums = lax.fori_loop(0, PIX // 512, add, jnp.zeros((n_rows, 128), F32))
         norm = 0.5 * jnp.sum(sums, axis=1, keepdims=True)
-
-        @pl.loop(0, 3)
-        def _(n):
-            rows = pl.ds(pl.multiple_of(n * 256, 256), 256)
-            part = lax.dot_general(
-                r(slice(None)), wim[rows, :], (((1,), (1,)), ((), ())), preferred_element_type=F32
-            )
-            out[:, rows] = part - norm
-
-    def do_scores(g):
-        scores(lambda cols: refs[g, :, cols], score.at[g], GROUP)
-        ex_send(g, score.at[g, :, theirs], core_in.at[g], core_pal)
-
-    def do_rows(g):
-        ex_wait(g, core_in.at[g])
-        row_out[g] = score[g, give, mine] + core_in[g, give, :]
-        ex_send(4 + g, row_out.at[g], row_in.at[g], hi_pal)
-        total[g] = score[g, keep, mine] + core_in[g, keep, :]
-
-    half_rows = (pl.ds(0, SIDE), pl.ds(SIDE, SIDE))
-
-    def do_scores_2(h):
-        def r(cols):
-            low = refs[2, h * 64 : h * 64 + 64, cols]
-            return jnp.concatenate([low, refs[2, SIDE + h * 64 : SIDE + h * 64 + 64, cols]], axis=0)
-
-        scores(r, score.at[2, half_rows[h]], SIDE)
-        n = (2, 10)[h]
-        ex_send(n, score.at[2, half_rows[h], theirs], core_in.at[2, half_rows[h]], core_pal)
-
-    def do_rows_2(h):
-        ex_wait((2, 10)[h], core_in.at[2, half_rows[h]])
-        block = 2 + 2 * h
-        row_out[block] = score[2, half_rows[h], mine] + core_in[2, half_rows[h], :]
-        ex_send((6, 11)[h], row_out.at[block], row_in.at[block], hi_pal)
-
-    def do_logits(block):
-        rows = pl.ds(block * SIDE, SIDE)
-        if block in (2, 4):
-            ex_wait({2: 6, 4: 11}[block], row_in.at[block])
-            summed = row_out[block] + row_in[block]
+        part = lax.dot_general(
+            of(slice(None)), wim[...], (((1,), (1,)), ((), ())), preferred_element_type=F32
+        )
+        score[slot_n, rows, :] = part - norm
+        ex_send(n, score.at[slot_n, rows, theirs], core_in.at[slot_n, rows], core_pal)
+
+    def do_rows(n):
+        slot_n, rows = places(n)
+        block, sums = sums_place(n)
+        ex_wait(n, core_in.at[slot_n, rows])
+        if n < 3:
+            row_out[block] = score[n, give, mine] + core_in[n, give, :]
+            total[block] = score[n, keep, mine] + core_in[n, keep, :]
         else:
-            ex_wait(4 + block, row_in.at[block])
-            summed = total[block] + row_in[block]
-        logits = INVERSE_HEAT * summed + prior[0, rows, :]
-        total[block] = logits
+            row_out[block, sums] = score[3, rows, mine] + core_in[3, rows, :]
+        ex_send(6 + n, row_out.at[block, sums], row_in.at[block, sums], hi_pal)
+
+    def do_logits(n):
+        block, sums = sums_place(n)
+        ex_wait(6 + n, row_in.at[block, sums])
+        near = total if n < 3 else row_out
+        first_row = FIRST[n]
+        size = SIDE if n < 3 else 2 * PIECE * len(BATCHES[n])
+        logits = INVERSE_HEAT * (near[block, sums] + row_in[block, sums])
+        logits = logits + prior[0, pl.ds(first_row, size), :]
+        total[block, sums] = logits
         return jnp.max(logits, axis=0, keepdims=True)
 
     def mass_of(blocks, top):
@@ -349,78 +382,69 @@
         return mass
 
     do_scores(0)
-    order = [(0, 0), (0, 1), (3, 0), (1, 0), (3, 1), (1, 1), (2, 0), (2, 1)]
-    forward = [(0, 0), (0, 1), (1, 0), (1, 1), (3, 0), (3, 1), (2, 0), (2, 1)]
-    arrived = []
-    passed = 0
-    for n, (b, yr) in enumerate(order):
-        for t in range(2):
-            ag_wait(("a+", t, b, yr), piece(t, 3, b, yr))
-            ag_wait(("a-", t, b, yr), piece(t, 1, b, yr))
-        arrived.append((b, yr))
-        while passed < 8 and forward[passed] in arrived:
-            b, yr = forward[passed]
-            for t in range(2):
-                ag_send(("af+", t, b, yr), piece(t, 3, b, yr, 0), piece(t, 2, b, yr, 0), a_plus[t])
-                ag_send(("af-", t, b, yr), piece(t, 1, b, yr, 1), piece(t, 2, b, yr, 1), a_minus[t])
-            passed += 1
-        if n == 1:
-            do_rows(0)
     do_scores(1)
+    pass_a(3, 1)
+    pass_a(1, 1)
+    do_rows(0)
+    do_rows(1)
+    opposite_landed(FORWARD[:4])
     do_scores(3)
-    do_rows(1)
+    pass_a(2, 0)
+    pass_a(2, 1)
     do_rows(3)
-
-    def opposite_landed(pieces):
-        for b, yr in pieces:
-            for t in range(2):
-                ag_wait(("af+", t, b, yr), piece(t, 2, b, yr, 0))
-                ag_wait(("af-", t, b, yr), piece(t, 2, b, yr, 1))
-
-    opposite_landed(forward[:4])
-    do_scores_2(0)
+    do_scores(2)
+    opposite_landed(FORWARD[4:6])
+    do_rows(2)
+    do_scores(4)
     top = do_logits(0)
-    do_rows_2(0)
-    opposite_landed(forward[4:])
-    do_scores_2(1)
     top = jnp.maximum(top, do_logits(1))
-    top = jnp.maximum(top, do_logits(3))
-    mass = mass_of((0, 1, 3), top)
+    do_rows(4)
+    opposite_landed(FORWARD[6:])
+    do_scores(5)
+    top = jnp.maximum(top, do_logits(2))
+    mass = mass_of((0, 1, 2), top)
     stat_out[0:1, :] = top
     stat_out[1:2, :] = mass
-    do_rows_2(1)
-    ex_send(8, stat_out.at[0:8], stat_in.at[0:8], hi_pal)
-    last_top = do_logits(2)
-    ex_wait(8, stat_in.at[0:8])
+    ex_send(12, stat_out.at[0:8], stat_in.at[0:8], hi_pal)
+    do_rows(5)
+    last_top = jnp.maximum(do_logits(3), do_logits(4))
+    ex_wait(12, stat_in.at[0:8])
     other_top, other_mass = stat_in[0:1, :], stat_in[1:2, :]
     first = y_hi == 0
     top_a, top_b = jnp.where(first, top, other_top), jnp.where(first, other_top, top)
     mass_a, mass_b = jnp.where(first, mass, other_mass), jnp.where(first, other_mass, mass)
-    last_top = jnp.maximum(last_top, do_logits(4))
+    last_top = jnp.maximum(last_top, do_logits(5))
     best = jnp.maximum(jnp.maximum(top_a, top_b), last_top)
     evidence = best + jnp.log(
-        mass_a * jnp.exp(top_a - best) + mass_b * jnp.exp(top_b - best) + mass_of((2, 4), best)
+        mass_a * jnp.exp(top_a - best) + mass_b * jnp.exp(top_b - best) + mass_of((3, 4), best)
     )
-    for h in range(2):
-        p = jnp.exp(total[2 + 2 * h] - evidence).astype(BF16)
-        for t in range(2):
-            rows = pl.ds(t * SIDE + h * 64, 64)
-            post[2, rows, mine] = p[t * 64 : t * 64 + 64, :]
-    ex_send(18, post.at[2, :, mine], post.at[2, :, mine], core_pal)
+    for n in (3, 4, 5):
+        block, sums = sums_place(n)
+        p = jnp.exp(total[block, sums] - evidence).astype(BF16)
+        for t in range(2):
+            for k, (g, b, yr) in enumerate(BATCHES[n]):
+                o = (t * len(BATCHES[n]) + k) * PIECE
+                rows = pl.ds(t * SIDE + b * 32 + yr * PIECE, PIECE)
+                post[g, rows, mine] = p[o : o + PIECE, :]
+    ex_send(20, post.at[2, :, mine], post.at[2, :, mine], core_pal)
     stat_out[8:16, :] = jnp.broadcast_to(evidence, (8, HALF))
-    for g in (1, 3, 0):
-        post[g, keep, mine] = jnp.exp(total[g] - evidence).astype(BF16)
-        ex_send(12 + g, post.at[g, keep, mine], post.at[g, keep, mine], hi_pal)
-        ex_send(16 + g, post.at[g, keep, mine], post.at[g, keep, mine], core_pal)
-    ex_send(9, stat_out.at[8:16], stat_in.at[8:16], core_pal)
+    for n in (1, 2, 0):
+        p = jnp.exp(total[n] - evidence).astype(BF16)
+        for k, (g, b, yr) in enumerate(BATCHES[n]):
+            first_row = pl.multiple_of(y_hi * SIDE + b * 32 + yr * PIECE, PIECE)
+            post[g, pl.ds(first_row, PIECE), mine] = p[k * PIECE : (k + 1) * PIECE, :]
+        for g in {1: (), 2: (1, 3), 0: (0,)}[n]:
+            ex_send(14 + g, post.at[g, keep, mine], post.at[g, keep, mine], hi_pal)
+            ex_send(18 + g, post.at[g, keep, mine], post.at[g, keep, mine], core_pal)
+    ex_send(13, stat_out.at[8:16], stat_in.at[8:16], core_pal)
 
     def do_relay(g):
-        ex_wait(12 + g, post.at[g, give, mine])
-        ex_send(20 + g, post.at[g, give, mine], post.at[g, give, mine], core_pal)
+        ex_wait(14 + g, post.at[g, give, mine])
+        ex_send(22 + g, post.at[g, give, mine], post.at[g, give, mine], core_pal)
 
     def do_posterior(g):
-        ex_wait(16 + g, post.at[g, keep, theirs])
-        ex_wait(20 + g, post.at[g, give, theirs])
+        ex_wait(18 + g, post.at[g, keep, theirs])
+        ex_wait(22 + g, post.at[g, give, theirs])
 
     def product(g, j):
         cols = pl.ds(pl.multiple_of(j * TILE, TILE), TILE)
@@ -458,7 +482,7 @@
     def get(src, j):
         return jnp.concatenate([src[j, a_rows(j, t)] for t in range(2)], axis=0).astype(F32)
 
-    ex_wait(18, post.at[2, :, theirs])
+    ex_wait(20, post.at[2, :, theirs])
 
     @pl.loop(0, 3)
     def _(k):
@@ -509,7 +533,7 @@
         for t in range(2):
             a_copy(2, k + 4, t, s3, r_plus, a_minus[t]).start()
 
-    ex_wait(9, stat_in.at[8:16])
+    ex_wait(13, stat_in.at[8:16])
     evid[:, mine] = stat_out[8:9, :]
     evid[:, theirs] = stat_in[8:9, :]
     for n in range(NIM // 128):
@@ -706,8 +730,8 @@
             dma((5,)),
             dma((84,)),
             dma((84,)),
-            dma((24,)),
-            dma((24,)),
+            dma((26,)),
+            dma((26,)),
             dma((3, NT, 2)),
             dma((3, NT, 2)),
             dma((3, NT, 2)),

time: 123 us -> 120 us (0.976)
  Pallas kernels: 119 us -> 116 us
    pallas_call x1, Pallas kernels: 119 us -> 116 us  [shards(): pl.pallas_call(kernel, out_shape=(jax.ShapeDtypeStruct((ROWS, PIX), F32),...]
where the time goes in v4:
time: 120 us
  Pallas kernels  116 us (97%)
  local copies, waits for them, and re-layouts  3.14 us (3%)
    pallas_call x1, Pallas kernels, shards(): pl.pallas_call(kernel, out_shape=(jax.ShapeDtypeStruct((ROWS, PIX), F32),...  116 us
    unnamed x2, local copies, waits for them, and re-layouts  3.14 us

profile of v4, /device:TPU:8, one launch (start us, length us, event | category | flops | bytes accessed | tf_op | source)
XLA Modules:
  0.0 119.6 jit_solution(17920583622644215323)
XLA Ops:
  0.6 115.8 %shard_map.95 = (f32[32,4096]{1,0:T(8,128)}, f32[6,128]{1,0:T(8,128)}) custom-call(bf16[768,4096]{1,0:T(8,128)(2,1)} %images_hbm.1, bf16[32,4096]{1,0:T(8,128)(2,1)} %references_hbm.1, s32[1,4096]{1,0:T(1,128)} %bitcast.7, f32[1,64]{1,0:T(1,128)} %bitcast.11, s32[8,128]{1,0:T(8,128)} %bitcast.9, s32[8,128]{1,0:T(8,128)} %bitcast.10, f32[1,6144]{1,0:T(1,128)} %bitcast.6, ...), custom_call_target="tpu_custom_call" | custom-call | tf_op jit(solution)/shard_map/pallas_call | solution.py:687
  116.4 1.9 %copy.12 = f32[32,4096]{1,0:T(8,128)} copy(f32[32,4096]{1,0:T(8,128)} %get-tuple-element.8) | data formatting | bytes 1048576
  118.3 1.3 %copy.13 = f32[768]{0:T(1024)} copy(f32[768]{0:T(1024)} %bitcast.8) | data formatting | bytes 6144

commit v5 on v4

--- a/solution.py
+++ b/solution.py
@@ -28,12 +28,15 @@
 BATCHES = [
     [(0, b, yr) for b, yr in FORWARD],
     [(g, b, yr) for g in (1, 3) for b, yr in FORWARD[:4]],
-    [(g, b, yr) for g in (1, 3) for b, yr in FORWARD[4:]],
+    [(g, b, yr) for g in (1, 3) for b, yr in FORWARD[4:6]],
+    [(g, b, yr) for g in (1, 3) for b, yr in FORWARD[6:]],
     [(2, b, yr) for b, yr in FORWARD[:4]],
     [(2, b, yr) for b, yr in FORWARD[4:6]],
     [(2, b, yr) for b, yr in FORWARD[6:]],
 ]
-FIRST = [0, SIDE, 2 * SIDE, 3 * SIDE, 4 * SIDE, 4 * SIDE + 64]
+SHARED = 4
+SCORE_ROW = [0, 256, 512, 640, 768, 896, 960]
+SUM_ROW = [0, 128, 256, 320, 384, 512, 576]
 
 
 def kernel(
@@ -202,11 +205,11 @@
 
         for n, batch in enumerate(BATCHES):
             for k, (g, b, yr) in enumerate(batch):
-                if n < 3:
-                    place(FIRST[n] + k * PIECE, g, b, yr, y_hi)
+                if n < SHARED:
+                    place(SUM_ROW[n] + k * PIECE, g, b, yr, y_hi)
                 else:
                     for t in range(2):
-                        place(FIRST[n] + (t * len(batch) + k) * PIECE, g, b, yr, t)
+                        place(SUM_ROW[n] + (t * len(batch) + k) * PIECE, g, b, yr, t)
 
         @pl.loop(0, 5)
         def _(block):
@@ -260,10 +263,11 @@
     for n in range(3):
         image_loads[n].wait()
 
-        @pl.loop(n * 16, n * 16 + 16)
+        @pl.loop(0, PIX // 256)
         def _(k):
-            rows = pl.ds(pl.multiple_of(k * 16, 16), 16)
-            wim[rows, :] = (im[rows, :].astype(F32) * weight[...]).astype(BF16)
+            cols = pl.ds(pl.multiple_of(k * 256, 256), 256)
+            rows = pl.ds(n * 256, 256)
+            wim[cols, rows] = (im[rows, cols].astype(F32) * weight[:, cols]).astype(BF16).T
 
     def pass_b(yr):
         for t in range(2):
@@ -315,18 +319,22 @@
     def ex_wait(n, dst):
         landed(dst, ex_s.at[n], ex_r.at[n])
 
-    def places(n):
-        rows = 2 * PIECE * len(BATCHES[n])
-        return (n, pl.ds(0, rows)) if n < 3 else (3, pl.ds(FIRST[n] - FIRST[3], rows))
-
-    def sums_place(n):
-        rows = SIDE if n < 3 else 2 * PIECE * len(BATCHES[n])
-        return (FIRST[n] // SIDE, pl.ds(FIRST[n] % SIDE, rows))
+    def size(n):
+        return 2 * PIECE * len(BATCHES[n])
+
+    def score_rows(n):
+        return pl.ds(SCORE_ROW[n], size(n))
+
+    def sum_rows(n):
+        return pl.ds(SUM_ROW[n], size(n) // 2 if n < SHARED else size(n))
+
+    def kind_rows(n, kind):
+        return pl.ds(pl.multiple_of(SCORE_ROW[n] + kind * (size(n) // 2), 16), size(n) // 2)
 
     def do_scores(n):
         batch = BATCHES[n]
-        n_rows = 2 * PIECE * len(batch)
-        slot_n, rows = places(n)
+        n_rows = size(n)
+        rows = score_rows(n)
 
         def of(cols):
             return jnp.concatenate(
@@ -338,113 +346,112 @@
                 axis=0,
             )
 
-        def add(k, sums):
-            for u in range(4):
-                cols = pl.ds(pl.multiple_of(k * 512 + u * 128, 128), 128)
+        def add(k, sums, chunks):
+            for u in range(chunks):
+                cols = pl.ds(pl.multiple_of((k * chunks + u) * 128, 128), 128)
                 part = of(cols).astype(F32)
                 sums = sums + part * part * weight[:, cols]
             return sums
 
-        sums = lax.fori_loop(0, PIX // 512, add, jnp.zeros((n_rows, 128), F32))
+        zero = jnp.zeros((n_rows, 128), F32)
+        if n_rows > 128:
+            sums = lax.fori_loop(0, PIX // 512, lambda k, v: add(k, v, 4), zero)
+        else:
+            sums = add(0, zero, PIX // 256) + add(1, zero, PIX // 256)
         norm = 0.5 * jnp.sum(sums, axis=1, keepdims=True)
-        part = lax.dot_general(
-            of(slice(None)), wim[...], (((1,), (1,)), ((), ())), preferred_element_type=F32
-        )
-        score[slot_n, rows, :] = part - norm
-        ex_send(n, score.at[slot_n, rows, theirs], core_in.at[slot_n, rows], core_pal)
+        part = jnp.dot(of(slice(None)), wim[...], preferred_element_type=F32)
+        score[rows, :] = part - norm
+        ex_send(n, score.at[rows, theirs], core_in.at[rows], core_pal)
 
     def do_rows(n):
-        slot_n, rows = places(n)
-        block, sums = sums_place(n)
-        ex_wait(n, core_in.at[slot_n, rows])
-        if n < 3:
-            row_out[block] = score[n, give, mine] + core_in[n, give, :]
-            total[block] = score[n, keep, mine] + core_in[n, keep, :]
+        rows, sums = score_rows(n), sum_rows(n)
+        ex_wait(n, core_in.at[rows])
+        if n < SHARED:
+            away, home = kind_rows(n, 1 - y_hi), kind_rows(n, y_hi)
+            row_out[sums] = score[away, mine] + core_in[away, :]
+            ex_send(7 + n, row_out.at[sums], row_in.at[sums], hi_pal)
+            total[sums] = score[home, mine] + core_in[home, :]
         else:
-            row_out[block, sums] = score[3, rows, mine] + core_in[3, rows, :]
-        ex_send(6 + n, row_out.at[block, sums], row_in.at[block, sums], hi_pal)
+            row_out[sums] = score[rows, mine] + core_in[rows, :]
+            ex_send(7 + n, row_out.at[sums], row_in.at[sums], hi_pal)
 
     def do_logits(n):
-        block, sums = sums_place(n)
-        ex_wait(6 + n, row_in.at[block, sums])
-        near = total if n < 3 else row_out
-        first_row = FIRST[n]
-        size = SIDE if n < 3 else 2 * PIECE * len(BATCHES[n])
-        logits = INVERSE_HEAT * (near[block, sums] + row_in[block, sums])
-        logits = logits + prior[0, pl.ds(first_row, size), :]
-        total[block, sums] = logits
+        sums = sum_rows(n)
+        ex_wait(7 + n, row_in.at[sums])
+        near = total if n < SHARED else row_out
+        logits = INVERSE_HEAT * (near[sums] + row_in[sums]) + prior[0, sums, :]
+        total[sums] = logits
         return jnp.max(logits, axis=0, keepdims=True)
 
-    def mass_of(blocks, top):
-        mass = jnp.zeros((1, HALF), F32)
-        for block in blocks:
-            mass = mass + jnp.sum(jnp.exp(total[block] - top), axis=0, keepdims=True)
-        return mass
-
+    def mass_of(rows, top):
+        return jnp.sum(jnp.exp(total[rows] - top), axis=0, keepdims=True)
+
+    shared_rows = pl.ds(0, 3 * SIDE)
     do_scores(0)
     do_scores(1)
+    do_rows(0)
+    do_rows(1)
     pass_a(3, 1)
     pass_a(1, 1)
-    do_rows(0)
-    do_rows(1)
+    do_scores(2)
     opposite_landed(FORWARD[:4])
-    do_scores(3)
+    do_scores(4)
+    do_rows(2)
+    do_rows(4)
     pass_a(2, 0)
     pass_a(2, 1)
+    do_scores(3)
+    opposite_landed(FORWARD[4:6])
     do_rows(3)
-    do_scores(2)
-    opposite_landed(FORWARD[4:6])
-    do_rows(2)
-    do_scores(4)
-    top = do_logits(0)
-    top = jnp.maximum(top, do_logits(1))
-    do_rows(4)
+    do_scores(5)
+    top = jnp.maximum(do_logits(0), do_logits(1))
     opposite_landed(FORWARD[6:])
-    do_scores(5)
+    do_rows(5)
+    do_scores(6)
     top = jnp.maximum(top, do_logits(2))
-    mass = mass_of((0, 1, 2), top)
+    top = jnp.maximum(top, do_logits(3))
+    mass = mass_of(shared_rows, top)
     stat_out[0:1, :] = top
     stat_out[1:2, :] = mass
-    ex_send(12, stat_out.at[0:8], stat_in.at[0:8], hi_pal)
-    do_rows(5)
-    last_top = jnp.maximum(do_logits(3), do_logits(4))
-    ex_wait(12, stat_in.at[0:8])
+    ex_send(14, stat_out.at[0:8], stat_in.at[0:8], hi_pal)
+    do_rows(6)
+    last_top = jnp.maximum(do_logits(4), do_logits(5))
+    ex_wait(14, stat_in.at[0:8])
     other_top, other_mass = stat_in[0:1, :], stat_in[1:2, :]
     first = y_hi == 0
     top_a, top_b = jnp.where(first, top, other_top), jnp.where(first, other_top, top)
     mass_a, mass_b = jnp.where(first, mass, other_mass), jnp.where(first, other_mass, mass)
-    last_top = jnp.maximum(last_top, do_logits(5))
+    last_top = jnp.maximum(last_top, do_logits(6))
     best = jnp.maximum(jnp.maximum(top_a, top_b), last_top)
     evidence = best + jnp.log(
-        mass_a * jnp.exp(top_a - best) + mass_b * jnp.exp(top_b - best) + mass_of((3, 4), best)
+        mass_a * jnp.exp(top_a - best) + mass_b * jnp.exp(top_b - best) + mass_of(pl.ds(3 * SIDE, 2 * SIDE), best)
     )
-    for n in (3, 4, 5):
-        block, sums = sums_place(n)
-        p = jnp.exp(total[block, sums] - evidence).astype(BF16)
+    for n in range(SHARED, len(BATCHES)):
+        p = jnp.exp(total[sum_rows(n)] - evidence).astype(BF16)
         for t in range(2):
             for k, (g, b, yr) in enumerate(BATCHES[n]):
                 o = (t * len(BATCHES[n]) + k) * PIECE
                 rows = pl.ds(t * SIDE + b * 32 + yr * PIECE, PIECE)
                 post[g, rows, mine] = p[o : o + PIECE, :]
-    ex_send(20, post.at[2, :, mine], post.at[2, :, mine], core_pal)
+    ex_send(22, post.at[2, :, mine], post.at[2, :, mine], core_pal)
     stat_out[8:16, :] = jnp.broadcast_to(evidence, (8, HALF))
-    for n in (1, 2, 0):
-        p = jnp.exp(total[n] - evidence).astype(BF16)
+    for n in (1, 2, 3, 0):
+        p = jnp.exp(total[sum_rows(n)] - evidence).astype(BF16)
         for k, (g, b, yr) in enumerate(BATCHES[n]):
             first_row = pl.multiple_of(y_hi * SIDE + b * 32 + yr * PIECE, PIECE)
             post[g, pl.ds(first_row, PIECE), mine] = p[k * PIECE : (k + 1) * PIECE, :]
-        for g in {1: (), 2: (1, 3), 0: (0,)}[n]:
-            ex_send(14 + g, post.at[g, keep, mine], post.at[g, keep, mine], hi_pal)
-            ex_send(18 + g, post.at[g, keep, mine], post.at[g, keep, mine], core_pal)
-    ex_send(13, stat_out.at[8:16], stat_in.at[8:16], core_pal)
+        for g in {3: (1, 3), 0: (0,)}.get(n, ()):
+            ex_send(16 + g, post.at[g, keep, mine], post.at[g, keep, mine], hi_pal)
+            ex_send(20 + g, post.at[g, keep, mine], post.at[g, keep, mine], core_pal)
+    ex_send(15, stat_out.at[8:16], stat_in.at[8:16], core_pal)
 
     def do_relay(g):
-        ex_wait(14 + g, post.at[g, give, mine])
-        ex_send(22 + g, post.at[g, give, mine], post.at[g, give, mine], core_pal)
+        ex_wait(16 + g, post.at[g, give, mine])
+        ex_send(24 + g, post.at[g, give, mine], post.at[g, give, mine], core_pal)
 
     def do_posterior(g):
-        ex_wait(18 + g, post.at[g, keep, theirs])
-        ex_wait(22 + g, post.at[g, give, theirs])
+        ex_wait(20 + g, post.at[g, keep, theirs])
+        ex_wait(24 + g, post.at[g, give, theirs])
 
     def product(g, j):
         cols = pl.ds(pl.multiple_of(j * TILE, TILE), TILE)
@@ -482,7 +489,7 @@
     def get(src, j):
         return jnp.concatenate([src[j, a_rows(j, t)] for t in range(2)], axis=0).astype(F32)
 
-    ex_wait(20, post.at[2, :, theirs])
+    ex_wait(22, post.at[2, :, theirs])
 
     @pl.loop(0, 3)
     def _(k):
@@ -495,45 +502,48 @@
 
     for n in range(2):
         first_product(2, n)
+    def free(k):
+        s1[k + 4] = product(1, k + 4).astype(BF16)
+        for t in range(2):
+            a_copy(1, k + 4, t, s1, r_minus, a_plus[t]).start()
+        s3[k] = product(3, k).astype(BF16)
+        for t in range(2):
+            a_copy(2, k, t, s3, r_plus, a_minus[t]).start()
+
+    def bound(k):
+        p1 = product(1, k)
+        for t in range(2):
+            a_landed(0, k, t, r_opp)
+        s1[k] = (p1 + r_opp[k].astype(F32)).astype(BF16)
+        for t in range(2):
+            a_copy(1, k, t, s1, r_minus, a_plus[t]).start()
+        p3 = product(3, k + 4)
+        for t in range(2):
+            a_landed(0, k + 4, t, r_opp)
+        s3[k + 4] = (p3 + r_opp[k + 4].astype(F32)).astype(BF16)
+        for t in range(2):
+            a_copy(2, k + 4, t, s3, r_plus, a_minus[t]).start()
+
     do_relay(1)
     do_relay(3)
     do_posterior(1)
     do_posterior(3)
-
-    @pl.loop(0, 3)
-    def _(k):
-        s1[k + 4] = product(1, k + 4).astype(BF16)
-        for t in range(2):
-            a_copy(1, k + 4, t, s1, r_minus, a_plus[t]).start()
-        s3[k] = product(3, k).astype(BF16)
-        for t in range(2):
-            a_copy(2, k, t, s3, r_plus, a_minus[t]).start()
-
     first_product(1, 1)
     first_product(3, 0)
     first_product(1, 0)
     first_product(3, 1)
+    free(0)
+
+    @pl.loop(0, 2)
+    def _(k):
+        bound(k)
+
     do_relay(0)
     do_posterior(0)
     for n in range(2):
         first_product(0, n)
 
-    @pl.loop(0, 3)
-    def _(k):
-        p1 = product(1, k)
-        for t in range(2):
-            a_landed(0, k, t, r_opp)
-        s1[k] = (p1 + r_opp[k].astype(F32)).astype(BF16)
-        for t in range(2):
-            a_copy(1, k, t, s1, r_minus, a_plus[t]).start()
-        p3 = product(3, k + 4)
-        for t in range(2):
-            a_landed(0, k + 4, t, r_opp)
-        s3[k + 4] = (p3 + r_opp[k + 4].astype(F32)).astype(BF16)
-        for t in range(2):
-            a_copy(2, k + 4, t, s3, r_plus, a_minus[t]).start()
-
-    ex_wait(13, stat_in.at[8:16])
+    ex_wait(15, stat_in.at[8:16])
     evid[:, mine] = stat_out[8:9, :]
     evid[:, theirs] = stat_in[8:9, :]
     for n in range(NIM // 128):
@@ -639,23 +649,30 @@
                 rows = slice(t * PIECE, (t + 1) * PIECE)
                 out_ref[rows, cols] = out_ref[rows, cols] + y_in[j, t].astype(F32)
 
+    step_a(0)
     first_opposite()
-    step_a(0)
+
+    @pl.loop(1, 3)
+    def _(k):
+        free(k)
+
+    bound(2)
     first_free()
     step_a(1)
     step_b(0)
+    step_a(2)
     first_bound()
-    step_a(2)
+    step_c(0)
     step_b(1)
+    step_b(2)
     step_a(3)
-    step_b(2)
-    step_c(0)
-    step_b(3)
     step_c(1)
     step_c(2)
+    step_b(3)
+    step_d(0)
+    step_d(1)
     step_c(3)
-    for k in range(3):
-        step_d(k)
+    step_d(2)
 
     for c in ag_sends:
         c.wait_send()
@@ -675,6 +692,17 @@
     for n in range(2):
         for g in range(4):
             f_copy(g, n).wait_send()
+
+
+def hand_over(sums_hbm, evidence_hbm, sums_out, evidence_out, sums, evidence, sems):
+    sources, held = (sums_hbm, evidence_hbm), (sums, evidence)
+    for n, out in enumerate((sums_out, evidence_out)):
+        pltpu.make_async_copy(sources[n], held[n], sems.at[0, n]).start()
+    for n, out in enumerate((sums_out, evidence_out)):
+        pltpu.make_async_copy(sources[n], held[n], sems.at[0, n]).wait()
+        pltpu.make_async_copy(held[n], out, sems.at[1, n]).start()
+    for n, out in enumerate((sums_out, evidence_out)):
+        pltpu.make_async_copy(held[n], out, sems.at[1, n]).wait()
 
 
 def shards(
@@ -694,13 +722,13 @@
         out_specs=(vmem, vmem),
         scratch_shapes=[
             pltpu.VMEM((NIM, PIX), BF16),
-            pltpu.VMEM((NIM, PIX), BF16),
+            pltpu.VMEM((PIX, NIM), BF16),
             pltpu.VMEM((4, GROUP, PIX), BF16),
-            pltpu.VMEM((4, GROUP, NIM), F32),
-            pltpu.VMEM((4, GROUP, HALF), F32),
-            pltpu.VMEM((5, SIDE, HALF), F32),
-            pltpu.VMEM((5, SIDE, HALF), F32),
-            pltpu.VMEM((5, SIDE, HALF), F32),
+            pltpu.VMEM((NREF, NIM), F32),
+            pltpu.VMEM((NREF, HALF), F32),
+            pltpu.VMEM((5 * SIDE, HALF), F32),
+            pltpu.VMEM((5 * SIDE, HALF), F32),
+            pltpu.VMEM((5 * SIDE, HALF), F32),
             pltpu.VMEM((1, PIX), F32),
             pltpu.VMEM((128, 128), F32),
             pltpu.VMEM((2, 128, 128), F32),
@@ -730,8 +758,8 @@
             dma((5,)),
             dma((84,)),
             dma((84,)),
-            dma((26,)),
-            dma((26,)),
+            dma((28,)),
+            dma((28,)),
             dma((3, NT, 2)),
             dma((3, NT, 2)),
             dma((3, NT, 2)),
@@ -742,7 +770,7 @@
             dma((2, 4)),
         ],
         compiler_params=pltpu.CompilerParams(
-            collective_id=0, has_side_effects=True, vmem_limit_bytes=67043328
+            collective_id=0, has_side_effects=True, vmem_limit_bytes=58 << 20
         ),
     )(
         images,
@@ -754,6 +782,20 @@
         orient_logw.reshape(1, NORIENT),
         class_logw,
     )
+    accumulators, evidence = pl.pallas_call(
+        hand_over,
+        out_shape=(
+            jax.ShapeDtypeStruct((ROWS, PIX), F32),
+            jax.ShapeDtypeStruct((NIM // 128, 128), F32),
+        ),
+        in_specs=[pl.BlockSpec(memory_space=pltpu.HBM)] * 2,
+        out_specs=(pl.BlockSpec(memory_space=pltpu.HBM),) * 2,
+        scratch_shapes=[
+            pltpu.VMEM((ROWS, PIX), F32),
+            pltpu.VMEM((NIM // 128, 128), F32),
+            dma((2, 2)),
+        ],
+    )(accumulators, evidence)
     return accumulators, evidence.reshape(NIM)
 
 

time: 120 us -> 117 us (0.975)
  local copies, waits for them, and re-layouts: 3.14 us -> 0 us
    unnamed x2 -> x0, local copies, waits for them, and re-layouts: 3.14 us -> none
    pallas_call x1, Pallas kernels: 116 us -> 113 us  [shards(): pl.pallas_call(kernel, out_shape=(jax.ShapeDtypeStruct((ROWS, PIX), F32),...]
    pallas_call x0 -> x1, Pallas kernels: none -> 1.87 us  [shards(): pl.pallas_call(hand_over, out_shape=(jax.ShapeDtypeStruct((ROWS, PIX), F3...]
where the time goes in v5:
time: 117 us; the launch traced here: 115 us
  Pallas kernels  115 us (98%)
    pallas_call x1, Pallas kernels, shards(): pl.pallas_call(kernel, out_shape=(jax.ShapeDtypeStruct((ROWS, PIX), F32),...  113 us

profile of v5, /device:TPU:8, one launch (start us, length us, event | category | flops | bytes accessed | tf_op | source)
XLA Modules:
  0.0 115.4 jit_solution(2594342421716928714)
XLA Ops:
  0.6 112.7 %shard_map.95 = (f32[32,4096]{1,0:T(8,128)}, f32[6,128]{1,0:T(8,128)}) custom-call(bf16[768,4096]{1,0:T(8,128)(2,1)} %images_hbm.1, bf16[32,4096]{1,0:T(8,128)(2,1)} %references_hbm.1, s32[1,4096]{1,0:T(1,128)} %bitcast.7, f32[1,64]{1,0:T(1,128)} %bitcast.10, s32[8,128]{1,0:T(8,128)} %bitcast.8, s32[8,128]{1,0:T(8,128)} %bitcast.9, f32[1,6144]{1,0:T(1,128)} %bitcast.6, ...), custom_call_target="tpu_custom_call" | custom-call | tf_op jit(solution)/shard_map/pallas_call | solution.py:715
  113.4 1.9 %shard_map.96 = (f32[32,4096]{1,0:T(8,128)}, f32[6,128]{1,0:T(8,128)}) custom-call(f32[32,4096]{1,0:T(8,128)} %get-tuple-element.6.sums_hbm, f32[6,128]{1,0:T(8,128)} %get-tuple-element.7.evidence_hbm), custom_call_target="tpu_custom_call" | custom-call | tf_op jit(solution)/shard_map/pallas_call | solution.py:785

commit v6 on v5

--- a/solution.py
+++ b/solution.py
@@ -257,7 +257,6 @@
     for t in range(2):
         ag_wait(("y", t), piece(t, 0, 0, 1))
         send_b(t, 1)
-    for t in range(2):
         send_a(t, 0, 1)
 
     for n in range(3):
@@ -293,10 +292,10 @@
                 ag_wait(("af-", t, b, yr), piece(t, 2, b, yr, 1))
 
     pass_b(0)
-    log_prior()
     pass_a(0, 0)
     pass_a(0, 1)
     pass_b(1)
+    log_prior()
     pass_a(3, 0)
     pass_a(1, 0)
     for yr in range(2):

time: 117 us -> 117 us (level)
  no operation moved by 1% of the time
where the time goes in v6:
time: 117 us; the launch traced here: 115 us
  Pallas kernels  114 us (97%)
    pallas_call x1, Pallas kernels, shards(): pl.pallas_call(kernel, out_shape=(jax.ShapeDtypeStruct((ROWS, PIX), F32),...  112 us

profile of v6, /device:TPU:8, one launch (start us, length us, event | category | flops | bytes accessed | tf_op | source)
XLA Modules:
  0.0 114.9 jit_solution(17949134329503948010)
XLA Ops:
  0.6 112.2 %shard_map.95 = (f32[32,4096]{1,0:T(8,128)}, f32[6,128]{1,0:T(8,128)}) custom-call(bf16[768,4096]{1,0:T(8,128)(2,1)} %images_hbm.1, bf16[32,4096]{1,0:T(8,128)(2,1)} %references_hbm.1, s32[1,4096]{1,0:T(1,128)} %bitcast.7, f32[1,64]{1,0:T(1,128)} %bitcast.10, s32[8,128]{1,0:T(8,128)} %bitcast.8, s32[8,128]{1,0:T(8,128)} %bitcast.9, f32[1,6144]{1,0:T(1,128)} %bitcast.6, ...), custom_call_target="tpu_custom_call" | custom-call | tf_op jit(solution)/shard_map/pallas_call | solution.py:714
  112.8 1.9 %shard_map.96 = (f32[32,4096]{1,0:T(8,128)}, f32[6,128]{1,0:T(8,128)}) custom-call(f32[32,4096]{1,0:T(8,128)} %get-tuple-element.6.sums_hbm, f32[6,128]{1,0:T(8,128)} %get-tuple-element.7.evidence_hbm), custom_call_target="tpu_custom_call" | custom-call | tf_op jit(solution)/shard_map/pallas_call | solution.py:784

commit v7 on v6

--- a/solution.py
+++ b/solution.py
@@ -259,6 +259,32 @@
         send_b(t, 1)
         send_a(t, 0, 1)
 
+    def pass_b(yr):
+        for t in range(2):
+            ag_wait(("b+", t, yr), piece(t, 0, 3, yr))
+            ag_send(("bf+", t, yr), piece(t, 0, 3, yr, 0), piece(t, 0, 2, yr, 0), b_plus[t])
+            ag_wait(("b-", t, yr), piece(t, 0, 1, yr))
+            ag_send(("bf-", t, yr), piece(t, 0, 1, yr, 1), piece(t, 0, 2, yr, 1), b_minus[t])
+        for t in range(2):
+            send_a(t, 3, yr)
+            send_a(t, 1, yr)
+
+    def pass_a(b, yr):
+        for t in range(2):
+            ag_wait(("a+", t, b, yr), piece(t, 3, b, yr))
+            ag_send(("af+", t, b, yr), piece(t, 3, b, yr, 0), piece(t, 2, b, yr, 0), a_plus[t])
+            ag_wait(("a-", t, b, yr), piece(t, 1, b, yr))
+            ag_send(("af-", t, b, yr), piece(t, 1, b, yr, 1), piece(t, 2, b, yr, 1), a_minus[t])
+
+    def opposite_landed(pieces):
+        for b, yr in pieces:
+            for t in range(2):
+                ag_wait(("af+", t, b, yr), piece(t, 2, b, yr, 0))
+                ag_wait(("af-", t, b, yr), piece(t, 2, b, yr, 1))
+
+    pass_b(0)
+    pass_a(0, 0)
+
     for n in range(3):
         image_loads[n].wait()
 
@@ -268,31 +294,6 @@
             rows = pl.ds(n * 256, 256)
             wim[cols, rows] = (im[rows, cols].astype(F32) * weight[:, cols]).astype(BF16).T
 
-    def pass_b(yr):
-        for t in range(2):
-            ag_wait(("b+", t, yr), piece(t, 0, 3, yr))
-            ag_send(("bf+", t, yr), piece(t, 0, 3, yr, 0), piece(t, 0, 2, yr, 0), b_plus[t])
-            ag_wait(("b-", t, yr), piece(t, 0, 1, yr))
-            ag_send(("bf-", t, yr), piece(t, 0, 1, yr, 1), piece(t, 0, 2, yr, 1), b_minus[t])
-        for t in range(2):
-            send_a(t, 3, yr)
-            send_a(t, 1, yr)
-
-    def pass_a(b, yr):
-        for t in range(2):
-            ag_wait(("a+", t, b, yr), piece(t, 3, b, yr))
-            ag_send(("af+", t, b, yr), piece(t, 3, b, yr, 0), piece(t, 2, b, yr, 0), a_plus[t])
-            ag_wait(("a-", t, b, yr), piece(t, 1, b, yr))
-            ag_send(("af-", t, b, yr), piece(t, 1, b, yr, 1), piece(t, 2, b, yr, 1), a_minus[t])
-
-    def opposite_landed(pieces):
-        for b, yr in pieces:
-            for t in range(2):
-                ag_wait(("af+", t, b, yr), piece(t, 2, b, yr, 0))
-                ag_wait(("af-", t, b, yr), piece(t, 2, b, yr, 1))
-
-    pass_b(0)
-    pass_a(0, 0)
     pass_a(0, 1)
     pass_b(1)
     log_prior()

time: 117 us -> 116 us (level)
  no operation moved by 1% of the time
where the time goes in v7:
time: 116 us; the launch traced here: 115 us
  Pallas kernels  114 us (98%)
    pallas_call x1, Pallas kernels, shards(): pl.pallas_call(kernel, out_shape=(jax.ShapeDtypeStruct((ROWS, PIX), F32),...  112 us

profile of v7, /device:TPU:8, one launch (start us, length us, event | category | flops | bytes accessed | tf_op | source)
XLA Modules:
  0.0 114.8 jit_solution(8280509866079509184)
XLA Ops:
  0.6 112.2 %shard_map.95 = (f32[32,4096]{1,0:T(8,128)}, f32[6,128]{1,0:T(8,128)}) custom-call(bf16[768,4096]{1,0:T(8,128)(2,1)} %images_hbm.1, bf16[32,4096]{1,0:T(8,128)(2,1)} %references_hbm.1, s32[1,4096]{1,0:T(1,128)} %bitcast.7, f32[1,64]{1,0:T(1,128)} %bitcast.10, s32[8,128]{1,0:T(8,128)} %bitcast.8, s32[8,128]{1,0:T(8,128)} %bitcast.9, f32[1,6144]{1,0:T(1,128)} %bitcast.6, ...), custom_call_target="tpu_custom_call" | custom-call | tf_op jit(solution)/shard_map/pallas_call | solution.py:715
  112.8 1.9 %shard_map.96 = (f32[32,4096]{1,0:T(8,128)}, f32[6,128]{1,0:T(8,128)}) custom-call(f32[32,4096]{1,0:T(8,128)} %get-tuple-element.6.sums_hbm, f32[6,128]{1,0:T(8,128)} %get-tuple-element.7.evidence_hbm), custom_call_target="tpu_custom_call" | custom-call | tf_op jit(solution)/shard_map/pallas_call | solution.py:785
